TPU v7x, 128 devices: a whole 4x4x4 slice. The times are simulated.
128 devices in a mesh: gx: 8 (over y_lo, x), gy: 8 (over z, core), gz: 2 (over y_hi).
Axes of the slice: x: 4, y: 4 (y_hi: 2, y_lo: 2; y = y_hi * 2 + y_lo), z: 4, core: 2. Of those that a mesh axis runs over, the one named last changes fastest.
Arguments:
- blocks: int32 [131072, 4], P(('gx', 'gy', 'gz')), may hold values from 0 to 15, as said below
- coefficients: bfloat16 [131072, 4, 128], P(('gx', 'gy', 'gz')), may hold values from -80 to 80
- residuals: float32 [131072], P(('gx', 'gy', 'gz')), may hold values from -3000 to 3000
Outputs:
- factor: float32 [8, 2, 128, 8, 2, 128], P('gx', None, None, 'gy')
- solution: float32 [16, 128], replicated
Inputs may be any that keep to these rules, and one draw needn't show every extreme that they name: Each row names 4 different blocks.
All inputs are finite; a program needn't handle non-finite values.
Results may differ from a plain program's by a relative error of at most 0.0003.
Values sent between devices are 32-bit elements; how exact they have to be, the bound alone decides.
A program may use at most 128 MiB of HBM per device.

v0:
```python
import jax
import jax.numpy as jnp
from jax import lax
from jax.sharding import PartitionSpec as P

G = 2048
BS = 128


def picked(x, axis, root):
    return lax.dynamic_index_in_dim(lax.all_gather(x, axis), root, 0, keepdims=False)


def laid_out(pieces, dim):
    shape = list(pieces.shape[1:])
    shape[dim] *= pieces.shape[0]
    return jnp.moveaxis(pieces, 0, dim).reshape(shape)


def copy_for_each(x, axis):
    size = lax.axis_size(axis)
    return lax.all_to_all(jnp.broadcast_to(x[None], (size, *x.shape)), axis, 0, 0, tiled=True)


def gather_directly(x, axis, dim):
    return laid_out(copy_for_each(x, axis), dim)


def on_device(blocks, coefficients, residuals):
    row_count = lax.axis_size("gx")
    col_count = lax.axis_size("gy")
    row_index = lax.axis_index("gx")
    col_index = lax.axis_index("gy")
    scale = 1.0 / (coefficients.shape[0] * row_count * col_count * lax.axis_size("gz"))
    width = coefficients.shape[2]
    nblock = G // BS
    per_dev = nblock // row_count
    target = (
        jnp.arange(per_dev, dtype=jnp.int32)[None, :] * row_count
        + jnp.arange(row_count, dtype=jnp.int32)[:, None]
    ).reshape(-1)
    placed = (blocks[:, :, None] == target[None, None, :]).astype(jnp.bfloat16)
    design = jnp.einsum("osz,osx->ozx", placed, coefficients, preferred_element_type=jnp.float32)
    design = design.astype(jnp.bfloat16).reshape(-1, row_count, per_dev, width)
    natural = (blocks[:, :, None] == jnp.arange(nblock, dtype=jnp.int32)[None, None, :]).astype(
        jnp.float32
    )
    weighted = coefficients.astype(jnp.float32) * residuals[:, None, None]
    rhs_local = (
        jnp.einsum("osb,osx->bx", natural, weighted, precision=lax.Precision.HIGHEST) * scale
    )
    rhs = lax.psum(rhs_local, ("gx", "gy", "gz"))
    row_span = min(row_count, (1 * lax.axis_size(("gx", "gy")) - 1) // col_count + 2)
    blockwise = (
        jnp.einsum("opix,oqjy->pqixjy", design, design, preferred_element_type=jnp.float32) * scale
    )
    blockwise = blockwise.reshape(row_span * col_count, per_dev, width, per_dev, width)
    summed = lax.psum_scatter(blockwise, ("gx", "gy"), scatter_dimension=0, tiled=True)
    summed = lax.psum(summed, "gz")
    matrix = summed.reshape(per_dev, width, per_dev, width)
    zero = jnp.zeros((), jnp.int32)
    block_ids = (
        jnp.arange(per_dev, dtype=jnp.int32)[None, :] * row_count
        + jnp.arange(row_count, dtype=jnp.int32)[:, None]
    )

    def factor_step(step, state):
        working, factor, pivots = state
        step_row = step % row_count
        step_local_row = step // row_count
        step_col = step % col_count
        step_local_col = step // col_count
        column = lax.dynamic_slice(
            working, (zero, zero, step_local_col, zero), (per_dev, width, 1, width)
        ).reshape(per_dev, width, width)
        row_raw = picked(column, "gy", step_col)
        whole = gather_directly(row_raw, "gx", 0).reshape(row_count, per_dev, width, width)
        own_diag = lax.dynamic_slice(
            whole, (step_row, step_local_row, zero, zero), (1, 1, width, width)
        ).reshape(width, width)
        chol = jnp.linalg.cholesky(own_diag)
        stacked = whole.transpose(3, 0, 1, 2).reshape(width, row_count * per_dev * width)
        solved = jax.scipy.linalg.solve_triangular(chol, stacked, lower=True)
        panel_all = solved.reshape(width, row_count, per_dev, width).transpose(1, 2, 3, 0)
        panel_all = jnp.where((block_ids > step)[:, :, None, None], panel_all, 0.0)
        row_panel = lax.dynamic_index_in_dim(panel_all, row_index, 0, keepdims=False)
        col_panel = lax.dynamic_index_in_dim(panel_all, col_index, 0, keepdims=False)
        working = working - jnp.einsum(
            "rxk,cyk->rxcy", row_panel, col_panel, precision=lax.Precision.HIGHEST
        )
        on_diag = (jnp.arange(per_dev, dtype=jnp.int32) == step_local_row) & (row_index == step_row)
        new_column = row_panel + jnp.where(on_diag[:, None, None], chol[None], 0.0)
        old_column = lax.dynamic_slice(
            factor, (zero, zero, step_local_col, zero), (per_dev, width, 1, width)
        ).reshape(per_dev, width, width)
        kept = jnp.where(col_index == step_col, new_column, old_column)
        factor = lax.dynamic_update_slice(
            factor, kept.reshape(per_dev, width, 1, width), (zero, zero, step_local_col, zero)
        )
        pivots = lax.dynamic_update_slice(pivots, chol[None], (step, zero, zero))
        return (working, factor, pivots)

    start_state = (matrix, jnp.zeros_like(matrix), jnp.zeros((nblock, width, width), jnp.float32))
    _, factor, pivots = lax.fori_loop(0, nblock, factor_step, start_state)
    shaped = factor.reshape(1, per_dev, width, 1, per_dev, width)
    across = lax.all_gather(shaped, "gy", axis=3, tiled=True)
    whole = lax.all_gather(across, "gx", axis=0, tiled=True)
    lower = whole.transpose(1, 0, 2, 4, 3, 5).reshape(nblock * width, nblock * width)
    middle = jax.scipy.linalg.solve_triangular(lower, rhs.reshape(-1), lower=True)
    answer = jax.scipy.linalg.solve_triangular(lower, middle, lower=True, trans=1)
    solution = answer.reshape(nblock, width)
    return (factor.reshape(1, per_dev, width, 1, per_dev, width), solution)


def solution(mesh):
    in_specs = (
        P(("gx", "gy", "gz"), None),
        P(("gx", "gy", "gz"), None, None),
        P(("gx", "gy", "gz")),
    )
    out_specs = (P("gx", None, None, "gy", None, None), P())
    return jax.shard_map(
        on_device, mesh=mesh, in_specs=in_specs, out_specs=out_specs, check_vma=False
    )
```

profile of v0, /device:TPU:1, one launch (start us, length us, event | category | flops | bytes accessed | tf_op | source)
XLA Modules:
  0.0 2133.1 jit_solution(3347520525819320981)
XLA Ops:
  25.3 16.4 copy.39
  42.0 311.7 %reduce-scatter.2.cloned.1.call-done = f32[1,2,128,2,128]{4,2,3,1,0:T(8,128)} async-done(((f32[64,2,128,2,128]{4,2,3,1,0:T(8,128)}), f32[1,2,128,2,128]{4,2,3,1,0:T(8,128)}) %reduce-scatter.2.cloned.1.call-update) | async-done | bytes 262160 | tf_op jit(solution)/shard_map/reduce_scatter | solution.py:58
  353.8 35.4 %all-reduce.2.cloned.1.call-done = f32[2,128,2,128]{3,1,2,0:T(8,128)} async-done(((f32[2,128,2,128]{3,1,2,0:T(8,128)}), f32[2,128,2,128]{3,1,2,0:T(8,128)}) %all-reduce.2.cloned.1.call-update) | async-done | bytes 262160 | tf_op jit(solution)/shard_map/psum | solution.py:59
  389.2 1176.2 %while.20 = (s32[]{:T(128)}, f32[2,128,2,128]{3,1,2,0:T(8,128)}, f32[2,128,2,128]{3,1,0,2:T(8,128)S(1)}, s32[]{:T(128)}, s32[]{:T(128)}, /*index=5*/s32[]{:T(128...) while((s32[]{:T(128)}, f32[2,128,2,128]{3,1,2,0:T(8,128)}, ...), condition=%wide.region_5.6_spmd.clone, body=%wide.region_2.5_spmd.clone.sunk | while | flops 503890112 | bytes 12519428 | solution.py:104
  391.0 25.2 %all-gather.13.cloned.1.call-done = f32[16,128,1,128]{3,1,2,0:T(8,128)} async-done(((f32[2,128,1,128]{3,1,2,0:T(8,128)}), f32[16,128,1,128]{3,1,2,0:T(8,128)}) %all-gather.13.cloned.1.call-update) | async-done | bytes 1048592 | tf_op jit(solution)/shard_map/while/body/eval_jaxpr/all_gather | solution.py:11
  423.0 15.8 all-to-all-done
  466.8 22.6 %all-gather.13.cloned.1.call-done = f32[16,128,1,128]{3,1,2,0:T(8,128)} async-done(((f32[2,128,1,128]{3,1,2,0:T(8,128)}), f32[16,128,1,128]{3,1,2,0:T(8,128)}) %all-gather.13.cloned.1.call-update) | async-done | bytes 1048592 | tf_op jit(solution)/shard_map/while/body/eval_jaxpr/all_gather | solution.py:11
  496.3 15.8 all-to-all-done
  540.0 22.6 %all-gather.13.cloned.1.call-done = f32[16,128,1,128]{3,1,2,0:T(8,128)} async-done(((f32[2,128,1,128]{3,1,2,0:T(8,128)}), f32[16,128,1,128]{3,1,2,0:T(8,128)}) %all-gather.13.cloned.1.call-update) | async-done | bytes 1048592 | tf_op jit(solution)/shard_map/while/body/eval_jaxpr/all_gather | solution.py:11
  569.5 15.8 all-to-all-done
  613.3 22.6 %all-gather.13.cloned.1.call-done = f32[16,128,1,128]{3,1,2,0:T(8,128)} async-done(((f32[2,128,1,128]{3,1,2,0:T(8,128)}), f32[16,128,1,128]{3,1,2,0:T(8,128)}) %all-gather.13.cloned.1.call-update) | async-done | bytes 1048592 | tf_op jit(solution)/shard_map/while/body/eval_jaxpr/all_gather | solution.py:11
  642.8 15.8 all-to-all-done
  686.5 22.9 %all-gather.13.cloned.1.call-done = f32[16,128,1,128]{3,1,2,0:T(8,128)} async-done(((f32[2,128,1,128]{3,1,2,0:T(8,128)}), f32[16,128,1,128]{3,1,2,0:T(8,128)}) %all-gather.13.cloned.1.call-update) | async-done | bytes 1048592 | tf_op jit(solution)/shard_map/while/body/eval_jaxpr/all_gather | solution.py:11
  716.4 15.8 all-to-all-done
  760.1 22.9 %all-gather.13.cloned.1.call-done = f32[16,128,1,128]{3,1,2,0:T(8,128)} async-done(((f32[2,128,1,128]{3,1,2,0:T(8,128)}), f32[16,128,1,128]{3,1,2,0:T(8,128)}) %all-gather.13.cloned.1.call-update) | async-done | bytes 1048592 | tf_op jit(solution)/shard_map/while/body/eval_jaxpr/all_gather | solution.py:11
  833.6 22.9 %all-gather.13.cloned.1.call-done = f32[16,128,1,128]{3,1,2,0:T(8,128)} async-done(((f32[2,128,1,128]{3,1,2,0:T(8,128)}), f32[16,128,1,128]{3,1,2,0:T(8,128)}) %all-gather.13.cloned.1.call-update) | async-done | bytes 1048592 | tf_op jit(solution)/shard_map/while/body/eval_jaxpr/all_gather | solution.py:11
  907.2 22.6 %all-gather.13.cloned.1.call-done = f32[16,128,1,128]{3,1,2,0:T(8,128)} async-done(((f32[2,128,1,128]{3,1,2,0:T(8,128)}), f32[16,128,1,128]{3,1,2,0:T(8,128)}) %all-gather.13.cloned.1.call-update) | async-done | bytes 1048592 | tf_op jit(solution)/shard_map/while/body/eval_jaxpr/all_gather | solution.py:11
  980.5 22.9 %all-gather.13.cloned.1.call-done = f32[16,128,1,128]{3,1,2,0:T(8,128)} async-done(((f32[2,128,1,128]{3,1,2,0:T(8,128)}), f32[16,128,1,128]{3,1,2,0:T(8,128)}) %all-gather.13.cloned.1.call-update) | async-done | bytes 1048592 | tf_op jit(solution)/shard_map/while/body/eval_jaxpr/all_gather | solution.py:11
  1054.0 22.6 %all-gather.13.cloned.1.call-done = f32[16,128,1,128]{3,1,2,0:T(8,128)} async-done(((f32[2,128,1,128]{3,1,2,0:T(8,128)}), f32[16,128,1,128]{3,1,2,0:T(8,128)}) %all-gather.13.cloned.1.call-update) | async-done | bytes 1048592 | tf_op jit(solution)/shard_map/while/body/eval_jaxpr/all_gather | solution.py:11
  1083.6 15.8 all-to-all-done
  1127.3 22.9 %all-gather.13.cloned.1.call-done = f32[16,128,1,128]{3,1,2,0:T(8,128)} async-done(((f32[2,128,1,128]{3,1,2,0:T(8,128)}), f32[16,128,1,128]{3,1,2,0:T(8,128)}) %all-gather.13.cloned.1.call-update) | async-done | bytes 1048592 | tf_op jit(solution)/shard_map/while/body/eval_jaxpr/all_gather | solution.py:11
  1200.8 22.6 %all-gather.13.cloned.1.call-done = f32[16,128,1,128]{3,1,2,0:T(8,128)} async-done(((f32[2,128,1,128]{3,1,2,0:T(8,128)}), f32[16,128,1,128]{3,1,2,0:T(8,128)}) %all-gather.13.cloned.1.call-update) | async-done | bytes 1048592 | tf_op jit(solution)/shard_map/while/body/eval_jaxpr/all_gather | solution.py:11
  1274.1 22.6 %all-gather.13.cloned.1.call-done = f32[16,128,1,128]{3,1,2,0:T(8,128)} async-done(((f32[2,128,1,128]{3,1,2,0:T(8,128)}), f32[16,128,1,128]{3,1,2,0:T(8,128)}) %all-gather.13.cloned.1.call-update) | async-done | bytes 1048592 | tf_op jit(solution)/shard_map/while/body/eval_jaxpr/all_gather | solution.py:11
  1347.4 22.6 %all-gather.13.cloned.1.call-done = f32[16,128,1,128]{3,1,2,0:T(8,128)} async-done(((f32[2,128,1,128]{3,1,2,0:T(8,128)}), f32[16,128,1,128]{3,1,2,0:T(8,128)}) %all-gather.13.cloned.1.call-update) | async-done | bytes 1048592 | tf_op jit(solution)/shard_map/while/body/eval_jaxpr/all_gather | solution.py:11
  1420.6 22.6 %all-gather.13.cloned.1.call-done = f32[16,128,1,128]{3,1,2,0:T(8,128)} async-done(((f32[2,128,1,128]{3,1,2,0:T(8,128)}), f32[16,128,1,128]{3,1,2,0:T(8,128)}) %all-gather.13.cloned.1.call-update) | async-done | bytes 1048592 | tf_op jit(solution)/shard_map/while/body/eval_jaxpr/all_gather | solution.py:11
  1450.1 15.8 all-to-all-done
  1493.9 22.6 %all-gather.13.cloned.1.call-done = f32[16,128,1,128]{3,1,2,0:T(8,128)} async-done(((f32[2,128,1,128]{3,1,2,0:T(8,128)}), f32[16,128,1,128]{3,1,2,0:T(8,128)}) %all-gather.13.cloned.1.call-update) | async-done | bytes 1048592 | tf_op jit(solution)/shard_map/while/body/eval_jaxpr/all_gather | solution.py:11
  1566.2 25.3 %all-gather.11.cloned.1.call-done = f32[2,128,16,128]{3,1,0,2:T(8,128)} async-done(((f32[2,128,2,128]{3,1,0,2:T(8,128)}), f32[2,128,16,128]{3,1,0,2:T(8,128)}) %all-gather.11.cloned.1.call-update) | async-done | bytes 2097168 | tf_op jit(solution)/shard_map/all_gather | solution.py:106
  1599.6 214.9 %psum.15 = f32[16,128]{1,0:T(8,128)S(1)} all-reduce(f32[16,128]{1,0:T(8,128)S(1)} %fusion.19), channel_id=1, replica_groups=mesh['gx'=8,'gy'=8,'gz'=2] {'gx','gy','gz'}, use_global_device_ids=true, to_apply=%region_6.7 | all-reduce | flops 2048 | bytes 16384 | tf_op jit(solution)/shard_map/psum | solution.py:52
  1827.8 18.0 reshape.532
  1858.2 56.3 %while.19 = (s32[]{:T(128)}, f32[2048,2048]{1,0:T(8,128)}, s32[16,2]{0,1:T(2,128)S(1)}, f32[16,128,128]{2,1,0:T(8,128)}, s32[]{:T(128)}) while((s32[]{:T(128)}, f32[2048,2048]{1,0:T(8,128)}, s32[16,2]{0,1:T(2,128)S(1)}, f32[16,128,128]{2,1,0:T(8,128)}, s32[]{:T(128)}) %tuple.184), condition=%wide.while_cond, body=%wide.while_body.sunk | while | flops 2 | bytes 132705 | solution.py:110
  1914.5 157.9 %custom-call.28 = f32[16,128,128]{1,2,0:T(8,128)S(1)} custom-call(f32[16,128,128]{2,1,0:T(8,128)} %get-tuple-element.183), custom_call_target="InvertDiagBlocksLowerTriangular" | custom-call | tf_op jit(solution)/shard_map/jit(_solve_triangular)/triangular_solve | solution.py:110
  (573 shorter events, 860.1 us)
Async XLA Ops:
  7.2 346.6 %reduce-scatter.2.cloned.1.call-start = ((), (), s32[]{:S(2)}) async-start(), calls=%async_computation.2 | async-start | bytes 17039360 | tf_op jit(solution)/shard_map/reduce_scatter | solution.py:58
  41.8 347.4 %all-reduce.2.cloned.1.call-start = ((), (), s32[]{:S(2)}) async-start(), calls=%async_computation.3 | async-start | bytes 524288 | tf_op jit(solution)/shard_map/psum | solution.py:59
  389.2 26.9 %all-gather.13.cloned.1.call-start = ((), (), s32[]{:S(2)}) async-start(), calls=%async_computation.6 | async-start | bytes 1179648 | tf_op jit(solution)/shard_map/while/body/eval_jaxpr/all_gather | solution.py:11
  418.1 20.8 all-to-all-start
  465.1 24.3 %all-gather.13.cloned.1.call-start = ((), (), s32[]{:S(2)}) async-start(), calls=%async_computation.6 | async-start | bytes 1179648 | tf_op jit(solution)/shard_map/while/body/eval_jaxpr/all_gather | solution.py:11
  538.3 24.3 %all-gather.13.cloned.1.call-start = ((), (), s32[]{:S(2)}) async-start(), calls=%async_computation.6 | async-start | bytes 1179648 | tf_op jit(solution)/shard_map/while/body/eval_jaxpr/all_gather | solution.py:11
  564.6 20.8 all-to-all-start
  611.6 24.3 %all-gather.13.cloned.1.call-start = ((), (), s32[]{:S(2)}) async-start(), calls=%async_computation.6 | async-start | bytes 1179648 | tf_op jit(solution)/shard_map/while/body/eval_jaxpr/all_gather | solution.py:11
  637.9 20.8 all-to-all-start
  684.8 24.6 %all-gather.13.cloned.1.call-start = ((), (), s32[]{:S(2)}) async-start(), calls=%async_computation.6 | async-start | bytes 1179648 | tf_op jit(solution)/shard_map/while/body/eval_jaxpr/all_gather | solution.py:11
  758.4 24.6 %all-gather.13.cloned.1.call-start = ((), (), s32[]{:S(2)}) async-start(), calls=%async_computation.6 | async-start | bytes 1179648 | tf_op jit(solution)/shard_map/while/body/eval_jaxpr/all_gather | solution.py:11
  785.0 20.8 all-to-all-start
  832.0 24.6 %all-gather.13.cloned.1.call-start = ((), (), s32[]{:S(2)}) async-start(), calls=%async_computation.6 | async-start | bytes 1179648 | tf_op jit(solution)/shard_map/while/body/eval_jaxpr/all_gather | solution.py:11
  858.6 20.8 all-to-all-start
  905.5 24.3 %all-gather.13.cloned.1.call-start = ((), (), s32[]{:S(2)}) async-start(), calls=%async_computation.6 | async-start | bytes 1179648 | tf_op jit(solution)/shard_map/while/body/eval_jaxpr/all_gather | solution.py:11
  978.8 24.6 %all-gather.13.cloned.1.call-start = ((), (), s32[]{:S(2)}) async-start(), calls=%async_computation.6 | async-start | bytes 1179648 | tf_op jit(solution)/shard_map/while/body/eval_jaxpr/all_gather | solution.py:11
  1005.4 20.8 all-to-all-start
  1052.4 24.3 %all-gather.13.cloned.1.call-start = ((), (), s32[]{:S(2)}) async-start(), calls=%async_computation.6 | async-start | bytes 1179648 | tf_op jit(solution)/shard_map/while/body/eval_jaxpr/all_gather | solution.py:11
  1078.6 20.8 all-to-all-start
  1125.6 24.6 %all-gather.13.cloned.1.call-start = ((), (), s32[]{:S(2)}) async-start(), calls=%async_computation.6 | async-start | bytes 1179648 | tf_op jit(solution)/shard_map/while/body/eval_jaxpr/all_gather | solution.py:11
  1152.2 20.8 all-to-all-start
  1199.2 24.3 %all-gather.13.cloned.1.call-start = ((), (), s32[]{:S(2)}) async-start(), calls=%async_computation.6 | async-start | bytes 1179648 | tf_op jit(solution)/shard_map/while/body/eval_jaxpr/all_gather | solution.py:11
  1225.4 20.8 all-to-all-start
  1272.4 24.3 %all-gather.13.cloned.1.call-start = ((), (), s32[]{:S(2)}) async-start(), calls=%async_computation.6 | async-start | bytes 1179648 | tf_op jit(solution)/shard_map/while/body/eval_jaxpr/all_gather | solution.py:11
  1298.7 20.8 all-to-all-start
  1345.7 24.3 %all-gather.13.cloned.1.call-start = ((), (), s32[]{:S(2)}) async-start(), calls=%async_computation.6 | async-start | bytes 1179648 | tf_op jit(solution)/shard_map/while/body/eval_jaxpr/all_gather | solution.py:11
  1372.0 20.8 all-to-all-start
  1418.9 24.3 %all-gather.13.cloned.1.call-start = ((), (), s32[]{:S(2)}) async-start(), calls=%async_computation.6 | async-start | bytes 1179648 | tf_op jit(solution)/shard_map/while/body/eval_jaxpr/all_gather | solution.py:11
  1445.2 20.8 all-to-all-start
  1492.2 24.3 %all-gather.13.cloned.1.call-start = ((), (), s32[]{:S(2)}) async-start(), calls=%async_computation.6 | async-start | bytes 1179648 | tf_op jit(solution)/shard_map/while/body/eval_jaxpr/all_gather | solution.py:11
  1565.4 26.1 %all-gather.11.cloned.1.call-start = ((), (), s32[]{:S(2)}) async-start(), calls=%async_computation.5 | async-start | bytes 2359296 | tf_op jit(solution)/shard_map/all_gather | solution.py:106
  1566.2 250.1 %all-gather.9.cloned.1.call-start = ((), (), s32[]{:S(2)}) async-start(), calls=%async_computation.4 | async-start | bytes 18874368 | tf_op jit(solution)/shard_map/all_gather | solution.py:107
  (9 other events, 3707.0 us)
Sparse Core Ops, SparseCore 0:
  41.9 311.8 reduce-scatter.1
  356.2 32.9 all-reduce.1
  392.3 23.7 all-gather.12
  467.9 21.4 all-gather.12
  541.1 21.4 all-gather.12
  614.4 21.4 all-gather.12
  688.0 21.4 all-gather.12
  761.5 21.4 all-gather.12
  835.1 21.4 all-gather.12
  908.3 21.4 all-gather.12
  981.9 21.4 all-gather.12
  1055.1 21.4 all-gather.12
  1128.7 21.4 all-gather.12
  1202.0 21.4 all-gather.12
  1275.2 21.4 all-gather.12
  1348.5 21.4 all-gather.12
  1421.7 21.4 all-gather.12
  1495.0 21.4 all-gather.12
  1568.0 23.5 all-gather.10
  1595.8 170.8 all-gather.8
where the time goes:
time: 2140 us; the launch traced here: 2130 us
  waiting for transfers between devices  992 us (46%)
  other arithmetic  543 us (25%)
  blocking collectives  215 us (10%)
  local copies, waits for them, and re-layouts  170 us (8%)
  matrix products  116 us (5%)
  starting transfers between devices  79.4 us (4%)
    all_gather x16, waiting for transfers between devices, picked(): lax.all_gather(x, axis)  366 us
    reduce_scatter x1, waiting for transfers between devices, on_device(): lax.psum_scatter(blockwise, ('gx', 'gy'), scatter_dimension=0, tiled=True)  312 us
    all_to_all x16, waiting for transfers between devices, copy_for_each(): lax.all_to_all(jnp.broadcast_to(x[None], (size, *x.shape)), axis, 0, 0, t...  253 us
    psum x1, blocking collectives, on_device(): rhs = lax.psum(rhs_local, ('gx', 'gy', 'gz'))  215 us
    another operation x48, other arithmetic, factor_step(): chol = jnp.linalg.cholesky(own_diag)  199 us
    another operation x3, other arithmetic, on_device(): jax.scipy.linalg.solve_triangular(lower, middle, lower=True, trans=1)  170 us
    another operation x32, other arithmetic, factor_step(): solved = jax.scipy.linalg.solve_triangular(chol, stacked, lower=True)  168 us
    all_to_all x16, starting transfers between devices, copy_for_each(): lax.all_to_all(jnp.broadcast_to(x[None], (size, *x.shape)), axis, 0, 0, t...  78.3 us
  transfers between devices with their start and end apart: 36, of which 35 were waited for; matrix products, arithmetic and copies ran while one was open for 0% of the time, Pallas kernels for 0%

commit v1 on v0

v1 whole, which is shorter than its diff:
```python
import functools

import jax
import jax.numpy as jnp
from jax import lax
from jax.experimental import pallas as pl
from jax.experimental.pallas import tpu as pltpu
from jax.sharding import PartitionSpec as P

G = 2048
BS = 128
SB = 2 * BS
NS = G // SB
EXTRA = 16
F32 = jnp.float32
BF16 = jnp.bfloat16
MESH = pl.DeviceIdType.MESH
TILES = [(i, j) for j in range(NS) for i in range(j, NS)]
ROWS = len(TILES) * SB
HALF = ROWS // 2
CHUNK = HALF // 3
ORDERS = ("xyz", "yzx", "zxy")


def gram_kernel(scale, blk_ref, coef_ref, res_ref, out_ref, design, flipped):
    obs = blk_ref.shape[0]
    slots = blk_ref.shape[1]
    step = 256

    def place(t, c):
        rows = pl.ds(pl.multiple_of(t * step, step), step)
        ids = [jnp.broadcast_to(blk_ref[rows, s : s + 1], (step, BS)) for s in range(slots)]
        vals = [coef_ref[rows, s * BS : (s + 1) * BS].astype(F32) for s in range(slots)]
        for b in range(G // BS):
            d = jnp.zeros((step, BS), F32)
            for s in range(slots):
                d = jnp.where(ids[s] == b, vals[s], d)
            db = d.astype(BF16)
            design[rows, b * BS : (b + 1) * BS] = db
            flipped[b * BS : (b + 1) * BS, rows] = db.T
        return c

    lax.fori_loop(0, obs // step, place, 0)

    res = res_ref[...]
    r1 = res.astype(BF16)
    rest = res - r1.astype(F32)
    r2 = rest.astype(BF16)
    r3 = (rest - r2.astype(F32)).astype(BF16)
    first = lax.broadcasted_iota(jnp.int32, (8, obs), 0)
    lhs = jnp.where(first == 0, r1.astype(F32), jnp.where(first == 1, r2.astype(F32), jnp.where(first == 2, r3.astype(F32), 0.0))).astype(BF16)

    for j in range(NS):
        base = TILES.index((j, j)) * SB
        cols = design[:, j * SB : (j + 1) * SB]

        def tile(i, c):
            rows = pl.ds(pl.multiple_of(i * SB, SB), SB)
            out = pl.ds(pl.multiple_of(base + (i - j) * SB, SB), SB)
            out_ref[out, :] = dot_nn(flipped[rows, :], cols) * scale
            return c

        lax.fori_loop(j, NS, tile, 0)
        side = jnp.sum(dot_nn(lhs, cols), axis=0, keepdims=True) * scale
        out_ref[base : base + 1, BS:] = side[:, :BS]
        out_ref[base + 1 : base + 2, BS:] = side[:, BS:]


def gram_call(blocks, coefficients, residuals, scale):
    obs = blocks.shape[0]
    return pl.pallas_call(
        functools.partial(gram_kernel, scale),
        out_shape=jax.ShapeDtypeStruct((ROWS, SB), F32),
        in_specs=[pl.BlockSpec(memory_space=pltpu.VMEM)] * 3,
        out_specs=pl.BlockSpec(memory_space=pltpu.VMEM),
        scratch_shapes=[pltpu.VMEM((obs, G), BF16), pltpu.VMEM((G, obs), BF16)],
        compiler_params=pltpu.CompilerParams(vmem_limit_bytes=60 * 1024 * 1024),
        name="gram",
    )(blocks, coefficients.reshape(obs, -1), residuals.reshape(1, obs))


def place_of(x, y, z, core):
    return (lax.rem(y, 2) * 4 + x, z * 2 + core, y // 2)


def reduce_kernel(in_ref, out_ref, work, near, far, core_sem, rs_sem, ag_sem, end_sem):
    gx, gy, gz = lax.axis_index("gx"), lax.axis_index("gy"), lax.axis_index("gz")
    at = {"x": lax.rem(gx, 4), "y": gz * 2 + gx // 4, "z": gy // 2}
    core = lax.rem(gy, 2)

    def device(axis=None, shift=0):
        c = dict(at)
        if axis is not None:
            c[axis] = lax.rem(c[axis] + shift + 4, 4)
        return place_of(c["x"], c["y"], c["z"], core)

    twin = place_of(at["x"], at["y"], at["z"], 1 - core)
    barrier = pltpu.get_barrier_semaphore()
    for axis in "xyz":
        for shift in (1, -1):
            pl.semaphore_signal(barrier, inc=1, device_id=device(axis, shift), device_id_type=MESH)
    pl.semaphore_signal(barrier, inc=1, device_id=twin, device_id_type=MESH)
    pl.semaphore_wait(barrier, 7)

    def remote(src, dst, sems, to):
        copy = pltpu.make_async_remote_copy(
            src_ref=src, dst_ref=dst, send_sem=sems.at[0], recv_sem=sems.at[1], device_id=to, device_id_type=MESH
        )
        copy.start()
        return copy

    mine = core * HALF
    other = (1 - core) * HALF
    pending = []

    def ds(start, size):
        return pl.ds(pl.multiple_of(start, 8), size)

    swaps = []
    for c in range(3):
        swaps.append(remote(in_ref.at[ds(other + c * CHUNK, CHUNK)], work.at[ds(c * CHUNK, CHUNK)], core_sem.at[c], twin))
    pending += swaps

    def add(dst, dst_start, src, src_start, size):
        step = 8 if size % 32 else 32

        def body(t, carry):
            d = ds(dst_start + t * step, step)
            dst[d, :] = dst[d, :] + src[ds(src_start + t * step, step), :]
            return carry

        lax.fori_loop(0, size // step, body, 0)

    bases = [c * CHUNK for c in range(3)]
    history = [[] for _ in range(3)]
    size = CHUNK
    offset = 0
    for p in range(3):
        unit = size // 4
        left = (unit // 2 + 7) // 8 * 8
        right = unit - left
        state = []
        for c in range(3):
            if p == 0:
                swaps[c].wait_recv()
                add(work, c * CHUNK, in_ref, mine + c * CHUNK, CHUNK)
            axis = ORDERS[c][p]
            m = at[axis]
            up, down = device(axis, 1), device(axis, -1)

            def piece(i, base=bases[c], m=m, unit=unit):
                return base + lax.rem(m + i + 4, 4) * unit

            half = near.at[c]
            a = remote(work.at[ds(piece(2), left)], half.at[ds(offset, left)], rs_sem.at[c, p, 0], up)
            b = remote(work.at[ds(piece(2) + left, right)], half.at[ds(offset + left, right)], rs_sem.at[c, p, 1], down)
            pending += [a, b]
            state.append((piece, up, down, a, b))
        ends = []
        for c in range(3):
            piece, up, down, a, b = state[c]
            a.wait_recv()
            add(work, piece(1), near.at[c], offset, left)
            u = remote(work.at[ds(piece(1), unit)], far.at[c, 0, ds(offset, unit)], rs_sem.at[c, p, 2], up)
            b.wait_recv()
            add(work, piece(-1) + left, near.at[c], offset + left, right)
            d = remote(work.at[ds(piece(-1), unit)], far.at[c, 1, ds(offset, unit)], rs_sem.at[c, p, 3], down)
            pending += [u, d]
            ends.append((u, d))
        for c in range(3):
            piece = state[c][0]
            for side in range(2):
                ends[c][side].wait_recv()
                add(work, piece(0), far.at[c, side], offset, unit)
            history[c].append((piece, state[c][1], state[c][2], unit, left, right))
            bases[c] = piece(0)
        offset += unit
        size = unit

    for c in range(3):
        unit = history[c][2][3]
        out_ref[ds(mine + bases[c], unit), :] = work[ds(bases[c], unit), :]
    for p in (2, 1, 0):
        firsts = []
        for c in range(3):
            piece, up, down, unit, left, right = history[c][p]
            own = out_ref.at[ds(mine + piece(0), unit)]
            u = remote(own, own, ag_sem.at[c, p, 0], up)
            d = remote(own, own, ag_sem.at[c, p, 1], down)
            pending += [u, d]
            firsts.append((u, d))
        seconds = []
        for c in range(3):
            piece, up, down, unit, left, right = history[c][p]
            firsts[c][0].wait_recv()
            part = out_ref.at[ds(mine + piece(-1), left)]
            u = remote(part, part, ag_sem.at[c, p, 2], up)
            firsts[c][1].wait_recv()
            part = out_ref.at[ds(mine + piece(1) + left, right)]
            d = remote(part, part, ag_sem.at[c, p, 3], down)
            pending += [u, d]
            seconds.append((u, d))
        for c in range(3):
            seconds[c][0].wait_recv()
            seconds[c][1].wait_recv()
    lasts = []
    for c in range(3):
        part = out_ref.at[ds(mine + c * CHUNK, CHUNK)]
        lasts.append(remote(part, part, end_sem.at[c], twin))
    for c in range(3):
        lasts[c].wait_recv()
    for copy in pending + lasts:
        copy.wait_send()


def reduce_call(payload):
    units = CHUNK // 4 + CHUNK // 16 + CHUNK // 64
    return pl.pallas_call(
        reduce_kernel,
        out_shape=jax.ShapeDtypeStruct((ROWS, SB), F32),
        in_specs=[pl.BlockSpec(memory_space=pltpu.VMEM)],
        out_specs=pl.BlockSpec(memory_space=pltpu.VMEM),
        scratch_shapes=[
            pltpu.VMEM((HALF, SB), F32),
            pltpu.VMEM((3, units, SB), F32),
            pltpu.VMEM((3, 2, units, SB), F32),
            pltpu.SemaphoreType.DMA((3, 2)),
            pltpu.SemaphoreType.DMA((3, 3, 4, 2)),
            pltpu.SemaphoreType.DMA((3, 3, 4, 2)),
            pltpu.SemaphoreType.DMA((3, 2)),
        ],
        compiler_params=pltpu.CompilerParams(
            vmem_limit_bytes=60 * 1024 * 1024, collective_id=0, has_side_effects=True
        ),
        name="reduce",
    )(payload)


def split(x):
    hi = x.astype(BF16)
    return hi, (x - hi.astype(F32)).astype(BF16)


def dot_nt(a, b):
    return lax.dot_general(a, b, (((1,), (1,)), ((), ())), preferred_element_type=F32)


def dot_nn(a, b):
    return lax.dot_general(a, b, (((1,), (0,)), ((), ())), preferred_element_type=F32)


def lane_all(x, lane):
    return jnp.broadcast_to(x[:, lane : lane + 1], x.shape)


def row_all(x, row):
    return jnp.broadcast_to(x[row : row + 1, :], x.shape)


def eliminate(w):
    lane = lax.broadcasted_iota(jnp.int32, (8, BS), 1)
    sub = lax.broadcasted_iota(jnp.int32, (8, BS), 0)
    w = list(w)
    for g in range(len(w)):
        r = w[g]
        cols = [lane_all(r, 8 * g + j) for j in range(8)]
        roots, rows, upper = [], [], []
        for j in range(8):
            root = lax.rsqrt(row_all(cols[j], j))
            below = jnp.where(sub > j, cols[j] * root, 0.0)
            here = lane == 8 * g + j
            row = row_all(jnp.where(here, 1.0, r), j) * root
            r = jnp.where(sub == j, row, jnp.where(here & (sub > j), 0.0, r) - below * row)
            ups = {}
            for l in range(j + 1, 8):
                ups[l] = row_all(cols[l], j) * root
                cols[l] = cols[l] - below * ups[l]
            roots.append(root)
            rows.append(jnp.where((lane > 8 * g + j) & (lane < 8 * g + 8), 0.0, row))
            upper.append(ups)
        w[g] = r
        group = (lane >= 8 * g) & (lane < 8 * g + 8)
        for i in range(g + 1, len(w)):
            c = [lane_all(w[i], 8 * g + j) for j in range(8)]
            acc = jnp.where(group, 0.0, w[i])
            for j in range(8):
                m = c[j] * roots[j]
                for l in range(j + 1, 8):
                    c[l] = c[l] - m * upper[j][l]
                acc = acc - m * rows[j]
            w[i] = acc
    return w


def chol_kernel(pos_ref, mat_ref, out_ref, sol_ref, a_ref, hi_ref, lo_ref, inv_ref, sem):
    n = G // BS
    copies = []
    for t, (i, j) in enumerate(TILES):
        copies.append(
            pltpu.make_async_copy(
                mat_ref.at[pl.ds(t * SB, SB)], a_ref.at[pl.ds(i * SB, SB), pl.ds(j * SB, SB)], sem.at[t]
            )
        )
        copies[-1].start()
    a_ref[pl.ds(G, EXTRA), :] = jnp.zeros((EXTRA, G), F32)
    for copy in copies:
        copy.wait()
    for j in range(NS):
        for h in range(2):
            a_ref[G : G + 1, j * SB + h * BS : j * SB + (h + 1) * BS] = a_ref[j * SB + h : j * SB + h + 1, j * SB + BS : (j + 1) * SB]
    lane2 = lax.broadcasted_iota(jnp.int32, (BS, BS), 1)
    sub2 = lax.broadcasted_iota(jnp.int32, (BS, BS), 0)

    def step(k, carry):
        at = pl.multiple_of(k * BS, BS)
        cols = pl.ds(at, BS)
        block = a_ref[pl.ds(at, BS), cols]
        w = eliminate([block[8 * i : 8 * i + 8] for i in range(BS // 8)])
        w = jnp.concatenate(w, axis=0)
        inv = jnp.where(lane2 <= sub2, w, 0.0)
        inv_ref[pl.ds(at, BS), :] = inv
        ih, il = split(inv)
        both = jnp.concatenate([ih, il], axis=0)
        diag = jnp.where(lane2 == sub2, 1.0 / w, jnp.where(lane2 > sub2, w, 0.0)).T
        a_ref[pl.ds(at, BS), cols] = diag
        dh, dl = split(diag)
        hi_ref[pl.ds(at, BS), cols] = dh
        lo_ref[pl.ds(at, BS), cols] = dl

        def solve(start, size):
            rows = pl.ds(start, size)
            xh, xl = split(a_ref[rows, cols])
            o = dot_nt(xh, both)
            o = o[:, :BS] + o[:, BS:] + dot_nt(xl, ih)
            a_ref[rows, cols] = o
            oh, ol = split(o)
            hi_ref[rows, cols] = oh
            lo_ref[rows, cols] = ol

        solve(G, EXTRA)
        odd = k % 2

        @pl.when(odd == 0)
        def _():
            solve(pl.multiple_of(at + BS, BS), BS)

        def solve_tile(t, c):
            solve(pl.multiple_of(t * 2 * BS, 2 * BS), 2 * BS)
            return c

        lax.fori_loop(k // 2 + 1, n // 2, solve_tile, 0)

        @pl.when(odd == 0)
        def _():
            nxt = pl.multiple_of(at + BS, BS)
            ncols = pl.ds(nxt, BS)
            bh = hi_ref[pl.ds(nxt, BS), cols]
            bl = lo_ref[pl.ds(nxt, BS), cols]
            bb = jnp.concatenate([bh, bl], axis=0)

            def update(start, size):
                rows = pl.ds(start, size)
                o = dot_nt(hi_ref[rows, cols], bb)
                o = o[:, :BS] + o[:, BS:] + dot_nt(lo_ref[rows, cols], bh)
                a_ref[rows, ncols] = a_ref[rows, ncols] - o

            update(G, EXTRA)
            update(nxt, BS)

            def tile(t, c):
                update(pl.multiple_of(t * 2 * BS, 2 * BS), 2 * BS)
                return c

            lax.fori_loop(k // 2 + 1, n // 2, tile, 0)

        @pl.when(odd == 1)
        def _():
            kk = k // 2
            pc = pl.ds(pl.multiple_of(kk * 2 * BS, 2 * BS), 2 * BS)

            def outer(jj, c):
                jc = pl.ds(pl.multiple_of(jj * 2 * BS, 2 * BS), 2 * BS)
                rh = hi_ref[jc, pc]
                rl = lo_ref[jc, pc]

                def update(rows):
                    xh = hi_ref[rows, pc]
                    xl = lo_ref[rows, pc]
                    o = dot_nt(xh, rh) + dot_nt(xl, rh) + dot_nt(xh, rl)
                    a_ref[rows, jc] = a_ref[rows, jc] - o

                update(pl.ds(G, EXTRA))

                def inner(ii, c2):
                    update(pl.ds(pl.multiple_of(ii * 2 * BS, 2 * BS), 2 * BS))
                    return c2

                lax.fori_loop(jj, n // 2, inner, 0)
                return c

            lax.fori_loop(kk + 1, n // 2, outer, 0)

        return carry

    lax.fori_loop(0, n, step, 0)

    def back(s, c):
        k = n - 1 - s
        at = pl.multiple_of(k * BS, BS)
        cols = pl.ds(at, BS)
        ih, il = split(inv_ref[pl.ds(at, BS), :])
        yh, yl = split(a_ref[pl.ds(G, EXTRA), cols])
        z = dot_nn(yh, ih) + dot_nn(yl, ih) + dot_nn(yh, il)
        sol_ref[:, cols] = z[:8]
        zh, zl = split(z)

        def sub(j, c2):
            jc = pl.ds(pl.multiple_of(j * BS, BS), BS)
            lh = hi_ref[pl.ds(at, BS), jc]
            ll = lo_ref[pl.ds(at, BS), jc]
            a_ref[pl.ds(G, EXTRA), jc] = a_ref[pl.ds(G, EXTRA), jc] - (dot_nn(zh, lh) + dot_nn(zl, lh) + dot_nn(zh, ll))
            return c2

        lax.fori_loop(0, k, sub, 0)
        return c

    lax.fori_loop(0, n, back, 0)

    p, q = pos_ref[0], pos_ref[1]
    for r in range(2):
        for c in range(2):
            rb = r * 8 + p
            cb = c * 8 + q
            blk = a_ref[pl.ds(pl.multiple_of(rb * BS, BS), BS), pl.ds(pl.multiple_of(cb * BS, BS), BS)]
            out_ref[r, :, c * BS : (c + 1) * BS] = jnp.where(rb >= cb, blk, 0.0)


def cholesky_call(pos, payload):
    return pl.pallas_call(
        chol_kernel,
        out_shape=(jax.ShapeDtypeStruct((2, BS, 2 * BS), F32), jax.ShapeDtypeStruct((8, G), F32)),
        in_specs=[
            pl.BlockSpec(memory_space=pltpu.SMEM),
            pl.BlockSpec(memory_space=pl.ANY),
        ],
        out_specs=(pl.BlockSpec(memory_space=pltpu.VMEM), pl.BlockSpec(memory_space=pltpu.VMEM)),
        scratch_shapes=[
            pltpu.VMEM((G + EXTRA, G), F32),
            pltpu.VMEM((G + EXTRA, G), BF16),
            pltpu.VMEM((G + EXTRA, G), BF16),
            pltpu.VMEM((G, BS), F32),
            pltpu.SemaphoreType.DMA((len(TILES),)),
        ],
        compiler_params=pltpu.CompilerParams(vmem_limit_bytes=60 * 1024 * 1024),
        name="chol",
    )(pos, payload)


def on_device(total, blocks, coefficients, residuals):
    payload = gram_call(blocks, coefficients, residuals, 1.0 / total)
    payload = reduce_call(payload)
    pos = jnp.stack([lax.axis_index("gx"), lax.axis_index("gy")]).astype(jnp.int32)
    factor, answer = cholesky_call(pos, payload)
    return factor.reshape(1, 2, BS, 1, 2, BS), answer[0].reshape(G // BS, BS)


def solution(mesh):
    def whole(blocks, coefficients, residuals):
        spread = P(("gx", "gy", "gz"))
        return jax.shard_map(
            functools.partial(on_device, blocks.shape[0]),
            mesh=mesh,
            in_specs=(spread, spread, spread),
            out_specs=(P("gx", None, None, "gy", None, None), P()),
            check_vma=False,
        )(blocks, coefficients, residuals)

    return whole
```

time: 2140 us -> 274 us (0.13)
  waiting for transfers between devices: 992 us -> 0 us
  other arithmetic: 543 us -> 0.59 us
  Pallas kernels: 0 us -> 265 us
  blocking collectives: 215 us -> 0 us
  local copies, waits for them, and re-layouts: 170 us -> 7.37 us
  matrix products: 116 us -> 0 us
  starting transfers between devices: 79.4 us -> 0 us
    another operation x83 -> x1, other arithmetic: 538 us -> 0.59 us  [on_device(): jnp.stack([lax.axis_index('gx'), lax.axis_index('gy')]).astype(jnp.int32)]
    all_gather x18 -> x0, waiting for transfers between devices: 391 us -> none  [the longest x16 366 us: picked(): lax.all_gather(x, axis)]
    reduce_scatter x1 -> x0, waiting for transfers between devices: 312 us -> none  [on_device(): lax.psum_scatter(blockwise, ('gx', 'gy'), scatter_dimension=0, tiled=True)]
    pallas_call x0 -> x3, Pallas kernels: none -> 265 us  [the longest x1 149 us: cholesky_call(): pl.pallas_call(chol_kernel, out_shape=(jax.ShapeDtypeStruct((2, BS, 2 * B...]
    all_to_all x16 -> x0, waiting for transfers between devices: 253 us -> none  [copy_for_each(): lax.all_to_all(jnp.broadcast_to(x[None], (size, *x.shape)), axis, 0, 0, t...]
    psum x1 -> x0, blocking collectives: 215 us -> none  [on_device(): rhs = lax.psum(rhs_local, ('gx', 'gy', 'gz'))]
    all_to_all x16 -> x0, starting transfers between devices: 78.3 us -> none  [copy_for_each(): lax.all_to_all(jnp.broadcast_to(x[None], (size, *x.shape)), axis, 0, 0, t...]
    another operation x78 -> x0, matrix products: 66.8 us -> none  [the longest x31 26.7 us: on_device(): jax.scipy.linalg.solve_triangular(lower, rhs.reshape(-1), lower=True)]
  transfers between devices with their start and end apart: 36 -> 0, of which waited for: 35 -> 0; matrix products, arithmetic and copies ran while one was open for 0% -> 0% of each run, Pallas kernels for 0% -> 0%
where the time goes in v1:
time: 274 us; the launch traced here: 273 us
  Pallas kernels  265 us (97%)
  local copies, waits for them, and re-layouts  7.37 us (3%)
    pallas_call x1, Pallas kernels, cholesky_call(): pl.pallas_call(chol_kernel, out_shape=(jax.ShapeDtypeStruct((2, BS, 2 * B...  149 us
    pallas_call x1, Pallas kernels, reduce_call(): pl.pallas_call(reduce_kernel, out_shape=jax.ShapeDtypeStruct((ROWS, SB),...  94.4 us
    pallas_call x1, Pallas kernels, gram_call(): pl.pallas_call(functools.partial(gram_kernel, scale), out_shape=jax.Shape...  20.9 us

profile of v1, /device:TPU:1, one launch (start us, length us, event | category | flops | bytes accessed | tf_op | source)
XLA Modules:
  0.0 273.4 jit_solution(9922228178616012294)
XLA Ops:
  0.6 0.6 pad_add_fusion.pos_ref
  1.2 1.8 copy.5.blk_ref
  3.0 2.4 copy.9
  5.4 20.9 %gram.1.in_ref = f32[9216,256]{1,0:T(8,128)} custom-call(s32[1024,4]{1,0:T(8,128)} %copy.5.blk_ref, bf16[1024,512]{1,0:T(8,128)(2,1)} %bitcast.9, f32[1,1024]{1,0:T(1,128)} %bitcast.13), custom_call_target="tpu_custom_call" | custom-call | tf_op jit(solution)/shard_map/gram/pallas_call | solution.py:71
  26.3 94.4 %reduce.1.mat_ref = f32[9216,256]{1,0:T(8,128)} custom-call(f32[9216,256]{1,0:T(8,128)} %gram.1.in_ref), custom_call_target="tpu_custom_call" | custom-call | tf_op jit(solution)/shard_map/reduce/pallas_call | solution.py:218
  120.8 149.5 %chol.1 = (f32[2,128,256]{2,1,0:T(8,128)}, f32[8,2048]{1,0:T(8,128)}) custom-call(s32[2]{0:T(128)} %pad_add_fusion.pos_ref, f32[9216,256]{1,0:T(8,128)} %reduce.1.mat_ref), custom_call_target="tpu_custom_call" | custom-call | tf_op jit(solution)/shard_map/chol/pallas_call | solution.py:439
  270.2 1.8 reshape.15
  272.0 1.4 slice.3

commit v2 on v1

--- a/solution.py
+++ b/solution.py
@@ -257,14 +257,54 @@
     return jnp.broadcast_to(x[row : row + 1, :], x.shape)
 
 
-def eliminate(w):
+NEAR = 3
+DUMMY = G + EXTRA
+TALL = DUMMY + SB + EXTRA
+UNITS = 7
+SIDES = NS - 1
+
+
+def plan():
+    n = 2 * NS
+    sides = [[DUMMY] * SIDES for _ in range(n)]
+    units = [[(DUMMY, 0, 0, 0)] * UNITS for _ in range(n)]
+    todo = []
+    for k in range(n):
+        if k:
+            first = (k - 1) // 2 + (1 if k % 2 else 2)
+            for t, i in enumerate(range(first, NS)):
+                sides[k][t] = i * SB
+        if k >= 2 and k % 2 == 0:
+            p = k // 2 - 1
+            for j in range(p + 1, NS):
+                for i in range(j, NS):
+                    if (i, j) != (p + 1, p + 1):
+                        todo.append((2 * j if i > j else 2 * j - 1, j, p, i))
+        todo.sort()
+        now, todo = todo[:UNITS], todo[UNITS:]
+        for t, (limit, j, p, i) in enumerate(now):
+            assert limit >= k
+            units[k][t] = (i * SB, j * SB, p * SB, 1 if i == j else 0)
+    assert not todo
+    flat = []
+    for k in range(n):
+        flat.append(sides[k] + [v for u in units[k] for v in u])
+    return flat
+
+
+def eliminate(w, fill):
     lane = lax.broadcasted_iota(jnp.int32, (8, BS), 1)
     sub = lax.broadcasted_iota(jnp.int32, (8, BS), 0)
     w = list(w)
-    for g in range(len(w)):
+    count = len(w)
+    cols = [lane_all(w[0], j) for j in range(8)]
+    for g in range(count):
         r = w[g]
-        cols = [lane_all(r, 8 * g + j) for j in range(8)]
-        roots, rows, upper = [], [], []
+        group = (lane >= 8 * g) & (lane < 8 * g + 8)
+        near = range(g + 1, min(g + 1 + NEAR, count))
+        raw = {i: [lane_all(w[i], 8 * g + j) for j in range(8)] for i in near}
+        ahead = [lane_all(w[g + 1], 8 * g + 8 + j) for j in range(8)] if g + 1 < count else None
+        accs = {i: jnp.where(group, 0.0, w[i]) for i in near}
         for j in range(8):
             root = lax.rsqrt(row_all(cols[j], j))
             below = jnp.where(sub > j, cols[j] * root, 0.0)
@@ -275,24 +315,50 @@
             for l in range(j + 1, 8):
                 ups[l] = row_all(cols[l], j) * root
                 cols[l] = cols[l] - below * ups[l]
-            roots.append(root)
-            rows.append(jnp.where((lane > 8 * g + j) & (lane < 8 * g + 8), 0.0, row))
-            upper.append(ups)
+            inverse_row = jnp.where((lane > 8 * g + j) & (lane < 8 * g + 8), 0.0, row)
+            for i in near:
+                c = raw[i]
+                m = c[j] * root
+                for l in range(j + 1, 8):
+                    c[l] = c[l] - m * ups[l]
+                accs[i] = accs[i] - m * inverse_row
+                if i == g + 1:
+                    ahead = [ahead[l] - m * row_all(m, l) for l in range(8)]
         w[g] = r
-        group = (lane >= 8 * g) & (lane < 8 * g + 8)
-        for i in range(g + 1, len(w)):
-            c = [lane_all(w[i], 8 * g + j) for j in range(8)]
-            acc = jnp.where(group, 0.0, w[i])
-            for j in range(8):
-                m = c[j] * roots[j]
-                for l in range(j + 1, 8):
-                    c[l] = c[l] - m * upper[j][l]
-                acc = acc - m * rows[j]
-            w[i] = acc
+        for i in near:
+            w[i] = accs[i]
+        far = g + 1 + NEAR
+        if far < count:
+            x = jnp.where(lane >= 8 * far, r, 0.0)
+            y = jnp.where(group & (lane > 8 * g + sub), 0.0, r)
+            xh = x.astype(BF16).astype(F32)
+            yh = y.astype(BF16).astype(F32)
+            zero = jnp.zeros_like(x)
+            xs = jnp.concatenate([xh, x - xh, xh, zero], axis=0).astype(BF16)
+            ys = jnp.concatenate([yh, yh, y - yh, zero], axis=0).astype(BF16)
+            delta = lax.dot_general(xs, ys, (((0,), (0,)), ((), ())), preferred_element_type=F32)
+            for i in range(far, count):
+                w[i] = jnp.where(group, 0.0, w[i]) - delta[8 * i : 8 * i + 8]
+        cols = ahead
+        fill(g)
     return w
 
 
-def chol_kernel(pos_ref, mat_ref, out_ref, sol_ref, a_ref, hi_ref, lo_ref, inv_ref, sem):
+def aligned(x, m=16):
+    return pl.multiple_of(x, m)
+
+
+def stacked(hi, lo):
+    return jnp.concatenate(
+        [jnp.concatenate([hi, hi], axis=1), jnp.concatenate([lo, jnp.zeros_like(lo)], axis=1)], axis=0
+    )
+
+
+def fold(o):
+    return o[:, :BS] + o[:, BS:]
+
+
+def chol_kernel(pos_ref, plan_ref, mat_ref, out_ref, sol_ref, a_ref, hi_ref, lo_ref, inv_ref, winv_ref, wnext_ref, sem):
     n = G // BS
     copies = []
     for t, (i, j) in enumerate(TILES):
@@ -307,121 +373,116 @@
         copy.wait()
     for j in range(NS):
         for h in range(2):
-            a_ref[G : G + 1, j * SB + h * BS : j * SB + (h + 1) * BS] = a_ref[j * SB + h : j * SB + h + 1, j * SB + BS : (j + 1) * SB]
+            a_ref[G : G + 1, j * SB + h * BS : j * SB + (h + 1) * BS] = a_ref[
+                j * SB + h : j * SB + h + 1, j * SB + BS : (j + 1) * SB
+            ]
     lane2 = lax.broadcasted_iota(jnp.int32, (BS, BS), 1)
     sub2 = lax.broadcasted_iota(jnp.int32, (BS, BS), 0)
+    ext = pl.ds(G, EXTRA)
+
+    def put(rows, cols, o):
+        oh, ol = split(o)
+        a_ref[rows, cols] = o
+        hi_ref[rows, cols] = oh
+        lo_ref[rows, cols] = ol
+        return jnp.concatenate([oh, ol], axis=1)
+
+    def solved(rows_list, cols):
+        x = jnp.concatenate([a_ref[rows, cols] for rows in rows_list], axis=0)
+        xh, xl = split(x)
+        return fold(dot_nt(jnp.concatenate([xh, xl], axis=1), winv_ref[...]))
+
+    def update(rows, erows, jc, pc):
+        xh = jnp.concatenate([hi_ref[rows, pc], hi_ref[ext, pc]], axis=0)
+        xl = jnp.concatenate([lo_ref[rows, pc], lo_ref[ext, pc]], axis=0)
+        rh, rl = hi_ref[jc, pc], lo_ref[jc, pc]
+        o = dot_nt(xh, rh) + dot_nt(xl, rh) + dot_nt(xh, rl)
+        a_ref[rows, jc] = a_ref[rows, jc] - o[:SB]
+        a_ref[erows, jc] = a_ref[erows, jc] - o[SB:]
 
     def step(k, carry):
-        at = pl.multiple_of(k * BS, BS)
+        at = aligned(k * BS, BS)
         cols = pl.ds(at, BS)
+        odd = lax.rem(k, 2)
+        prev = pl.ds(aligned(jnp.maximum(k - 1, 0) * BS, BS), BS)
+        edummy = DUMMY + SB
+        eside = pl.ds(aligned(jnp.where(odd == 1, G, edummy)), EXTRA)
+
+        def fill(g):
+            if g < SIDES:
+                base = plan_ref[k, g]
+                rows = pl.ds(aligned(base), SB)
+                o = solved([rows, eside] if g == 0 else [rows], prev)
+                both = put(rows, prev, o[:SB])
+                if g == 0:
+                    both = jnp.concatenate([both, put(eside, prev, o[SB:])], axis=0)
+                d = fold(dot_nt(both, wnext_ref[...]))
+                drows = pl.ds(aligned(jnp.where(odd == 1, base, DUMMY)), SB)
+                a_ref[drows, cols] = a_ref[drows, cols] - d[:SB]
+                if g == 0:
+                    a_ref[eside, cols] = a_ref[eside, cols] - d[SB:]
+            elif g < SIDES + UNITS:
+                u = SIDES + 4 * (g - SIDES)
+                rows = pl.ds(aligned(plan_ref[k, u]), SB)
+                jc = pl.ds(aligned(plan_ref[k, u + 1], SB), SB)
+                pc = pl.ds(aligned(plan_ref[k, u + 2], SB), SB)
+                update(rows, pl.ds(aligned(jnp.where(plan_ref[k, u + 3] == 1, G, edummy)), EXTRA), jc, pc)
+
         block = a_ref[pl.ds(at, BS), cols]
-        w = eliminate([block[8 * i : 8 * i + 8] for i in range(BS // 8)])
+        w = eliminate([block[8 * i : 8 * i + 8] for i in range(BS // 8)], fill)
         w = jnp.concatenate(w, axis=0)
         inv = jnp.where(lane2 <= sub2, w, 0.0)
         inv_ref[pl.ds(at, BS), :] = inv
         ih, il = split(inv)
-        both = jnp.concatenate([ih, il], axis=0)
-        diag = jnp.where(lane2 == sub2, 1.0 / w, jnp.where(lane2 > sub2, w, 0.0)).T
-        a_ref[pl.ds(at, BS), cols] = diag
-        dh, dl = split(diag)
-        hi_ref[pl.ds(at, BS), cols] = dh
-        lo_ref[pl.ds(at, BS), cols] = dl
-
-        def solve(start, size):
-            rows = pl.ds(start, size)
-            xh, xl = split(a_ref[rows, cols])
-            o = dot_nt(xh, both)
-            o = o[:, :BS] + o[:, BS:] + dot_nt(xl, ih)
-            a_ref[rows, cols] = o
-            oh, ol = split(o)
-            hi_ref[rows, cols] = oh
-            lo_ref[rows, cols] = ol
-
-        solve(G, EXTRA)
-        odd = k % 2
+        winv_ref[...] = stacked(ih, il)
 
         @pl.when(odd == 0)
         def _():
-            solve(pl.multiple_of(at + BS, BS), BS)
-
-        def solve_tile(t, c):
-            solve(pl.multiple_of(t * 2 * BS, 2 * BS), 2 * BS)
-            return c
-
-        lax.fori_loop(k // 2 + 1, n // 2, solve_tile, 0)
-
-        @pl.when(odd == 0)
+            nxt = pl.ds(aligned(at + BS, BS), BS)
+            o = solved([nxt], cols)
+            both = put(nxt, cols, o)
+            weights = stacked(both[:, :BS], both[:, BS:])
+            wnext_ref[...] = weights
+            a_ref[nxt, nxt] = a_ref[nxt, nxt] - fold(dot_nt(both, weights))
+
+        @pl.when((odd == 1) & (k < n - 1))
         def _():
-            nxt = pl.multiple_of(at + BS, BS)
-            ncols = pl.ds(nxt, BS)
-            bh = hi_ref[pl.ds(nxt, BS), cols]
-            bl = lo_ref[pl.ds(nxt, BS), cols]
-            bb = jnp.concatenate([bh, bl], axis=0)
-
-            def update(start, size):
-                rows = pl.ds(start, size)
-                o = dot_nt(hi_ref[rows, cols], bb)
-                o = o[:, :BS] + o[:, BS:] + dot_nt(lo_ref[rows, cols], bh)
-                a_ref[rows, ncols] = a_ref[rows, ncols] - o
-
-            update(G, EXTRA)
-            update(nxt, BS)
-
-            def tile(t, c):
-                update(pl.multiple_of(t * 2 * BS, 2 * BS), 2 * BS)
-                return c
-
-            lax.fori_loop(k // 2 + 1, n // 2, tile, 0)
-
-        @pl.when(odd == 1)
+            nxt = pl.ds(aligned(at + BS, BS), SB)
+            o = solved([nxt, ext], cols)
+            put(nxt, cols, o[:SB])
+            put(ext, cols, o[SB:])
+            update(nxt, ext, nxt, pl.ds(aligned(at - BS, SB), SB))
+
+        @pl.when(k == n - 1)
         def _():
-            kk = k // 2
-            pc = pl.ds(pl.multiple_of(kk * 2 * BS, 2 * BS), 2 * BS)
-
-            def outer(jj, c):
-                jc = pl.ds(pl.multiple_of(jj * 2 * BS, 2 * BS), 2 * BS)
-                rh = hi_ref[jc, pc]
-                rl = lo_ref[jc, pc]
-
-                def update(rows):
-                    xh = hi_ref[rows, pc]
-                    xl = lo_ref[rows, pc]
-                    o = dot_nt(xh, rh) + dot_nt(xl, rh) + dot_nt(xh, rl)
-                    a_ref[rows, jc] = a_ref[rows, jc] - o
-
-                update(pl.ds(G, EXTRA))
-
-                def inner(ii, c2):
-                    update(pl.ds(pl.multiple_of(ii * 2 * BS, 2 * BS), 2 * BS))
-                    return c2
-
-                lax.fori_loop(jj, n // 2, inner, 0)
-                return c
-
-            lax.fori_loop(kk + 1, n // 2, outer, 0)
-
+            put(ext, cols, solved([ext], cols))
+
+        put(pl.ds(at, BS), cols, jnp.where(lane2 == sub2, 1.0 / w, jnp.where(lane2 > sub2, w, 0.0)).T)
         return carry
 
     lax.fori_loop(0, n, step, 0)
 
     def back(s, c):
         k = n - 1 - s
-        at = pl.multiple_of(k * BS, BS)
+        at = aligned(k * BS, BS)
         cols = pl.ds(at, BS)
         ih, il = split(inv_ref[pl.ds(at, BS), :])
-        yh, yl = split(a_ref[pl.ds(G, EXTRA), cols])
-        z = dot_nn(yh, ih) + dot_nn(yl, ih) + dot_nn(yh, il)
-        sol_ref[:, cols] = z[:8]
+        yh, yl = split(a_ref[pl.ds(G, 8), cols])
+        y = jnp.concatenate([yh, yl], axis=0)
+        z = dot_nn(y, ih)
+        z = z[:8] + z[8:] + dot_nn(yh, il)
+        sol_ref[:, cols] = z
         zh, zl = split(z)
+        zz = jnp.concatenate([zh, zl], axis=0)
+        wide = 4 * BS
 
         def sub(j, c2):
-            jc = pl.ds(pl.multiple_of(j * BS, BS), BS)
-            lh = hi_ref[pl.ds(at, BS), jc]
-            ll = lo_ref[pl.ds(at, BS), jc]
-            a_ref[pl.ds(G, EXTRA), jc] = a_ref[pl.ds(G, EXTRA), jc] - (dot_nn(zh, lh) + dot_nn(zl, lh) + dot_nn(zh, ll))
+            jc = pl.ds(aligned(j * wide, wide), wide)
+            o = dot_nn(zz, hi_ref[pl.ds(at, BS), jc])
+            a_ref[pl.ds(G, 8), jc] = a_ref[pl.ds(G, 8), jc] - (o[:8] + o[8:] + dot_nn(zh, lo_ref[pl.ds(at, BS), jc]))
             return c2
 
-        lax.fori_loop(0, k, sub, 0)
+        lax.fori_loop(0, (k + 3) // 4, sub, 0)
         return c
 
     lax.fori_loop(0, n, back, 0)
@@ -431,7 +492,7 @@
         for c in range(2):
             rb = r * 8 + p
             cb = c * 8 + q
-            blk = a_ref[pl.ds(pl.multiple_of(rb * BS, BS), BS), pl.ds(pl.multiple_of(cb * BS, BS), BS)]
+            blk = a_ref[pl.ds(aligned(rb * BS, BS), BS), pl.ds(aligned(cb * BS, BS), BS)]
             out_ref[r, :, c * BS : (c + 1) * BS] = jnp.where(rb >= cb, blk, 0.0)
 
 
@@ -441,19 +502,22 @@
         out_shape=(jax.ShapeDtypeStruct((2, BS, 2 * BS), F32), jax.ShapeDtypeStruct((8, G), F32)),
         in_specs=[
             pl.BlockSpec(memory_space=pltpu.SMEM),
+            pl.BlockSpec(memory_space=pltpu.SMEM),
             pl.BlockSpec(memory_space=pl.ANY),
         ],
         out_specs=(pl.BlockSpec(memory_space=pltpu.VMEM), pl.BlockSpec(memory_space=pltpu.VMEM)),
         scratch_shapes=[
-            pltpu.VMEM((G + EXTRA, G), F32),
-            pltpu.VMEM((G + EXTRA, G), BF16),
-            pltpu.VMEM((G + EXTRA, G), BF16),
+            pltpu.VMEM((TALL, G), F32),
+            pltpu.VMEM((TALL, G), BF16),
+            pltpu.VMEM((TALL, G), BF16),
             pltpu.VMEM((G, BS), F32),
+            pltpu.VMEM((SB, SB), BF16),
+            pltpu.VMEM((SB, SB), BF16),
             pltpu.SemaphoreType.DMA((len(TILES),)),
         ],
         compiler_params=pltpu.CompilerParams(vmem_limit_bytes=60 * 1024 * 1024),
         name="chol",
-    )(pos, payload)
+    )(pos, jnp.asarray(plan(), jnp.int32), payload)
 
 
 def on_device(total, blocks, coefficients, residuals):

time: 274 us -> 212 us (0.77)
  Pallas kernels: 265 us -> 203 us
    pallas_call x1, Pallas kernels: 149 us -> 88 us  [cholesky_call(): pl.pallas_call(chol_kernel, out_shape=(jax.ShapeDtypeStruct((2, BS, 2 * B...]
where the time goes in v2:
time: 212 us
  Pallas kernels  203 us (96%)
  local copies, waits for them, and re-layouts  7.37 us (3%)
    pallas_call x1, Pallas kernels, reduce_call(): pl.pallas_call(reduce_kernel, out_shape=jax.ShapeDtypeStruct((ROWS, SB),...  94.4 us
    pallas_call x1, Pallas kernels, cholesky_call(): pl.pallas_call(chol_kernel, out_shape=(jax.ShapeDtypeStruct((2, BS, 2 * B...  88 us
    pallas_call x1, Pallas kernels, gram_call(): pl.pallas_call(functools.partial(gram_kernel, scale), out_shape=jax.Shape...  20.9 us

profile of v2, /device:TPU:1, one launch (start us, length us, event | category | flops | bytes accessed | tf_op | source)
XLA Modules:
  0.0 212.0 jit_solution(1172020749568229126)
XLA Ops:
  0.6 0.6 pad_add_fusion.pos_ref
  1.2 1.8 copy.6.blk_ref
  3.0 2.4 %copy.10 = bf16[128,8,4,128]{3,1,2,0:T(8,128)(2,1)} copy(bf16[128,8,4,128]{3,2,1,0:T(4,128)(2,1)} %bitcast.10) | data formatting | bytes 2097152
  5.4 20.9 %gram.1.in_ref = f32[9216,256]{1,0:T(8,128)} custom-call(s32[1024,4]{1,0:T(8,128)} %copy.6.blk_ref, bf16[1024,512]{1,0:T(8,128)(2,1)} %bitcast.9, f32[1,1024]{1,0:T(1,128)} %bitcast.13), custom_call_target="tpu_custom_call" | custom-call | tf_op jit(solution)/shard_map/gram/pallas_call | solution.py:71
  26.3 94.4 %reduce.1.mat_ref = f32[9216,256]{1,0:T(8,128)} custom-call(f32[9216,256]{1,0:T(8,128)} %gram.1.in_ref), custom_call_target="tpu_custom_call" | custom-call | tf_op jit(solution)/shard_map/reduce/pallas_call | solution.py:218
  120.8 88.0 %chol.1 = (f32[2,128,256]{2,1,0:T(8,128)}, f32[8,2048]{1,0:T(8,128)}) custom-call(s32[2]{0:T(128)} %pad_add_fusion.pos_ref, s32[16,35]{1,0:T(8,128)} %constant.12.clone.plan_ref, f32[9216,256]{1,0:T(8,128)} %reduce.1.mat_ref), custom_call_target="tpu_custom_call" | custom-call | tf_op jit(solution)/shard_map/chol/pallas_call | solution.py:500
  208.8 1.8 reshape.15
  210.6 1.4 slice.3

commit v3 on v2

--- a/solution.py
+++ b/solution.py
@@ -15,14 +15,65 @@
 F32 = jnp.float32
 BF16 = jnp.bfloat16
 MESH = pl.DeviceIdType.MESH
-TILES = [(i, j) for j in range(NS) for i in range(j, NS)]
+ROUNDS = 3
+STREAMS = 3 * ROUNDS
+DIAG = [(j, j) for j in range(NS)]
+SIDE = [(i, j) for j in range(NS) for i in range(j + 1, NS)]
+TILES = DIAG[0::2] + SIDE[0::2] + DIAG[1::2] + SIDE[1::2]
 ROWS = len(TILES) * SB
 HALF = ROWS // 2
-CHUNK = HALF // 3
+PART = HALF // STREAMS
+UNITS_OF = (PART // 4, PART // 16, PART // 64)
 ORDERS = ("xyz", "yzx", "zxy")
 
 
-def gram_kernel(scale, blk_ref, coef_ref, res_ref, out_ref, design, flipped):
+def split(x):
+    hi = x.astype(BF16)
+    return hi, (x - hi.astype(F32)).astype(BF16)
+
+
+def dot_nt(a, b):
+    return lax.dot_general(a, b, (((1,), (1,)), ((), ())), preferred_element_type=F32)
+
+
+def dot_nn(a, b):
+    return lax.dot_general(a, b, (((1,), (0,)), ((), ())), preferred_element_type=F32)
+
+
+def lane_all(x, lane):
+    return jnp.broadcast_to(x[:, lane : lane + 1], x.shape)
+
+
+def row_all(x, row):
+    return jnp.broadcast_to(x[row : row + 1, :], x.shape)
+
+
+def place_of(x, y, z, core):
+    return (lax.rem(y, 2) * 4 + x, z * 2 + core, y // 2)
+
+
+def halves(unit):
+    left = (unit // 2 + 7) // 8 * 8
+    return left, unit - left
+
+
+def reduce_kernel(scale, blk_ref, coef_ref, res_ref, pay, design, flipped, outbox, inbox, work, near, far, swap_sem, rs_sem, ag_sem, end_sem):
+    gx, gy, gz = lax.axis_index("gx"), lax.axis_index("gy"), lax.axis_index("gz")
+    at = {"x": lax.rem(gx, 4), "y": gz * 2 + gx // 4, "z": gy // 2}
+    core = lax.rem(gy, 2)
+
+    def device(axis, shift):
+        c = dict(at)
+        c[axis] = lax.rem(c[axis] + shift + 4, 4)
+        return place_of(c["x"], c["y"], c["z"], core)
+
+    twin = place_of(at["x"], at["y"], at["z"], 1 - core)
+    barrier = pltpu.get_barrier_semaphore()
+    for axis in "xyz":
+        for shift in (1, -1):
+            pl.semaphore_signal(barrier, inc=1, device_id=device(axis, shift), device_id_type=MESH)
+    pl.semaphore_signal(barrier, inc=1, device_id=twin, device_id_type=MESH)
+
     obs = blk_ref.shape[0]
     slots = blk_ref.shape[1]
     step = 256
@@ -43,218 +94,199 @@
     lax.fori_loop(0, obs // step, place, 0)
 
     res = res_ref[...]
-    r1 = res.astype(BF16)
-    rest = res - r1.astype(F32)
-    r2 = rest.astype(BF16)
-    r3 = (rest - r2.astype(F32)).astype(BF16)
+    r1 = res.astype(BF16).astype(F32)
+    r2 = (res - r1).astype(BF16).astype(F32)
+    r3 = res - r1 - r2
     first = lax.broadcasted_iota(jnp.int32, (8, obs), 0)
-    lhs = jnp.where(first == 0, r1.astype(F32), jnp.where(first == 1, r2.astype(F32), jnp.where(first == 2, r3.astype(F32), 0.0))).astype(BF16)
-
-    for j in range(NS):
-        base = TILES.index((j, j)) * SB
-        cols = design[:, j * SB : (j + 1) * SB]
-
-        def tile(i, c):
-            rows = pl.ds(pl.multiple_of(i * SB, SB), SB)
-            out = pl.ds(pl.multiple_of(base + (i - j) * SB, SB), SB)
-            out_ref[out, :] = dot_nn(flipped[rows, :], cols) * scale
-            return c
-
-        lax.fori_loop(j, NS, tile, 0)
-        side = jnp.sum(dot_nn(lhs, cols), axis=0, keepdims=True) * scale
-        out_ref[base : base + 1, BS:] = side[:, :BS]
-        out_ref[base + 1 : base + 2, BS:] = side[:, BS:]
-
-
-def gram_call(blocks, coefficients, residuals, scale):
-    obs = blocks.shape[0]
-    return pl.pallas_call(
-        functools.partial(gram_kernel, scale),
-        out_shape=jax.ShapeDtypeStruct((ROWS, SB), F32),
-        in_specs=[pl.BlockSpec(memory_space=pltpu.VMEM)] * 3,
-        out_specs=pl.BlockSpec(memory_space=pltpu.VMEM),
-        scratch_shapes=[pltpu.VMEM((obs, G), BF16), pltpu.VMEM((G, obs), BF16)],
-        compiler_params=pltpu.CompilerParams(vmem_limit_bytes=60 * 1024 * 1024),
-        name="gram",
-    )(blocks, coefficients.reshape(obs, -1), residuals.reshape(1, obs))
-
-
-def place_of(x, y, z, core):
-    return (lax.rem(y, 2) * 4 + x, z * 2 + core, y // 2)
-
-
-def reduce_kernel(in_ref, out_ref, work, near, far, core_sem, rs_sem, ag_sem, end_sem):
-    gx, gy, gz = lax.axis_index("gx"), lax.axis_index("gy"), lax.axis_index("gz")
-    at = {"x": lax.rem(gx, 4), "y": gz * 2 + gx // 4, "z": gy // 2}
-    core = lax.rem(gy, 2)
-
-    def device(axis=None, shift=0):
-        c = dict(at)
-        if axis is not None:
-            c[axis] = lax.rem(c[axis] + shift + 4, 4)
-        return place_of(c["x"], c["y"], c["z"], core)
-
-    twin = place_of(at["x"], at["y"], at["z"], 1 - core)
-    barrier = pltpu.get_barrier_semaphore()
-    for axis in "xyz":
-        for shift in (1, -1):
-            pl.semaphore_signal(barrier, inc=1, device_id=device(axis, shift), device_id_type=MESH)
-    pl.semaphore_signal(barrier, inc=1, device_id=twin, device_id_type=MESH)
-    pl.semaphore_wait(barrier, 7)
+    lhs = jnp.where(first == 0, r1, jnp.where(first == 1, r2, jnp.where(first == 2, r3, 0.0))).astype(BF16)
+
+    def ds(start, size):
+        return pl.ds(pl.multiple_of(start, 8), size)
+
+    mine = core * HALF
+
+    def gram(side, slot, dst):
+        (i0, j0), (i1, j1) = TILES[slot], TILES[slot + len(TILES) // 2]
+        i = (i0 + (i1 - i0) * side) * SB
+        j = (j0 + (j1 - j0) * side) * SB
+        cols = design[:, pl.ds(pl.multiple_of(j, SB), SB)]
+        base = slot * SB
+        dst[base : base + SB, :] = dot_nn(flipped[pl.ds(pl.multiple_of(i, SB), SB), :], cols) * scale
+        if i0 == j0:
+            row = jnp.sum(dot_nn(lhs, cols), axis=0, keepdims=True) * scale
+            dst[base : base + 8, BS:] = jnp.concatenate([row[:, :BS], row[:, BS:], jnp.zeros((6, BS), F32)], axis=0)
+
+    started = []
 
     def remote(src, dst, sems, to):
         copy = pltpu.make_async_remote_copy(
             src_ref=src, dst_ref=dst, send_sem=sems.at[0], recv_sem=sems.at[1], device_id=to, device_id_type=MESH
         )
         copy.start()
+        started.append(copy)
         return copy
 
-    mine = core * HALF
-    other = (1 - core) * HALF
-    pending = []
-
-    def ds(start, size):
-        return pl.ds(pl.multiple_of(start, 8), size)
-
-    swaps = []
-    for c in range(3):
-        swaps.append(remote(in_ref.at[ds(other + c * CHUNK, CHUNK)], work.at[ds(c * CHUNK, CHUNK)], core_sem.at[c], twin))
-    pending += swaps
-
     def add(dst, dst_start, src, src_start, size):
-        step = 8 if size % 32 else 32
+        piece = min(size, 64)
 
         def body(t, carry):
-            d = ds(dst_start + t * step, step)
-            dst[d, :] = dst[d, :] + src[ds(src_start + t * step, step), :]
+            d = ds(dst_start + t * piece, piece)
+            dst[d, :] = dst[d, :] + src[ds(src_start + t * piece, piece), :]
             return carry
 
-        lax.fori_loop(0, size // step, body, 0)
-
-    bases = [c * CHUNK for c in range(3)]
-    history = [[] for _ in range(3)]
-    size = CHUNK
-    offset = 0
-    for p in range(3):
-        unit = size // 4
-        left = (unit // 2 + 7) // 8 * 8
-        right = unit - left
-        state = []
-        for c in range(3):
+        if size == piece:
+            body(0, 0)
+        else:
+            lax.fori_loop(0, size // piece, body, 0)
+
+    class Stream:
+        def __init__(self, s):
+            self.s = s
+            self.order = ORDERS[s % 3]
+            self.base = s * PART
+            self.pieces = []
+
+        def swap(self):
+            rows = PART * self.s
+            self.swapped = remote(outbox.at[ds(rows, PART)], inbox.at[ds(rows, PART)], swap_sem.at[self.s], twin)
+
+        def opposite(self, p):
+            s, unit = self.s, UNITS_OF[p]
             if p == 0:
-                swaps[c].wait_recv()
-                add(work, c * CHUNK, in_ref, mine + c * CHUNK, CHUNK)
-            axis = ORDERS[c][p]
-            m = at[axis]
-            up, down = device(axis, 1), device(axis, -1)
-
-            def piece(i, base=bases[c], m=m, unit=unit):
-                return base + lax.rem(m + i + 4, 4) * unit
-
-            half = near.at[c]
-            a = remote(work.at[ds(piece(2), left)], half.at[ds(offset, left)], rs_sem.at[c, p, 0], up)
-            b = remote(work.at[ds(piece(2) + left, right)], half.at[ds(offset + left, right)], rs_sem.at[c, p, 1], down)
-            pending += [a, b]
-            state.append((piece, up, down, a, b))
-        ends = []
-        for c in range(3):
-            piece, up, down, a, b = state[c]
-            a.wait_recv()
-            add(work, piece(1), near.at[c], offset, left)
-            u = remote(work.at[ds(piece(1), unit)], far.at[c, 0, ds(offset, unit)], rs_sem.at[c, p, 2], up)
-            b.wait_recv()
-            add(work, piece(-1) + left, near.at[c], offset + left, right)
-            d = remote(work.at[ds(piece(-1), unit)], far.at[c, 1, ds(offset, unit)], rs_sem.at[c, p, 3], down)
-            pending += [u, d]
-            ends.append((u, d))
-        for c in range(3):
-            piece = state[c][0]
-            for side in range(2):
-                ends[c][side].wait_recv()
-                add(work, piece(0), far.at[c, side], offset, unit)
-            history[c].append((piece, state[c][1], state[c][2], unit, left, right))
-            bases[c] = piece(0)
-        offset += unit
-        size = unit
-
-    for c in range(3):
-        unit = history[c][2][3]
-        out_ref[ds(mine + bases[c], unit), :] = work[ds(bases[c], unit), :]
-    for p in (2, 1, 0):
-        firsts = []
-        for c in range(3):
-            piece, up, down, unit, left, right = history[c][p]
-            own = out_ref.at[ds(mine + piece(0), unit)]
-            u = remote(own, own, ag_sem.at[c, p, 0], up)
-            d = remote(own, own, ag_sem.at[c, p, 1], down)
-            pending += [u, d]
-            firsts.append((u, d))
-        seconds = []
-        for c in range(3):
-            piece, up, down, unit, left, right = history[c][p]
-            firsts[c][0].wait_recv()
-            part = out_ref.at[ds(mine + piece(-1), left)]
-            u = remote(part, part, ag_sem.at[c, p, 2], up)
-            firsts[c][1].wait_recv()
-            part = out_ref.at[ds(mine + piece(1) + left, right)]
-            d = remote(part, part, ag_sem.at[c, p, 3], down)
-            pending += [u, d]
-            seconds.append((u, d))
-        for c in range(3):
-            seconds[c][0].wait_recv()
-            seconds[c][1].wait_recv()
-    lasts = []
-    for c in range(3):
-        part = out_ref.at[ds(mine + c * CHUNK, CHUNK)]
-        lasts.append(remote(part, part, end_sem.at[c], twin))
-    for c in range(3):
-        lasts[c].wait_recv()
-    for copy in pending + lasts:
+                self.swapped.wait_recv()
+                add(work, PART * s, inbox, PART * s, PART)
+            else:
+                self.finish(p - 1)
+            axis = self.order[p]
+            m, base = at[axis], self.base
+            self.pieces.append(lambda i: base + lax.rem(m + i + 4, 4) * unit)
+            left, right = halves(unit)
+            piece, off = self.pieces[p], sum(UNITS_OF[:p])
+            self.a = remote(work.at[ds(piece(2), left)], near.at[s, ds(off, left)], rs_sem.at[s, p, 0], device(axis, 1))
+            if right:
+                self.b = remote(
+                    work.at[ds(piece(2) + left, right)], near.at[s, ds(off + left, right)], rs_sem.at[s, p, 1], device(axis, -1)
+                )
+
+        def sides(self, p):
+            s, unit, axis, piece = self.s, UNITS_OF[p], self.order[p], self.pieces[p]
+            left, right = halves(unit)
+            off = sum(UNITS_OF[:p])
+            self.a.wait_recv()
+            add(work, piece(1), near.at[s], off, left)
+            self.u = remote(work.at[ds(piece(1), unit)], far.at[s, 0, ds(off, unit)], rs_sem.at[s, p, 2], device(axis, 1))
+            if right:
+                self.b.wait_recv()
+                add(work, piece(-1) + left, near.at[s], off + left, right)
+            self.d = remote(work.at[ds(piece(-1), unit)], far.at[s, 1, ds(off, unit)], rs_sem.at[s, p, 3], device(axis, -1))
+
+        def finish(self, p):
+            s, unit, piece = self.s, UNITS_OF[p], self.pieces[p]
+            off = sum(UNITS_OF[:p])
+            for k, copy in enumerate((self.u, self.d)):
+                copy.wait_recv()
+                add(work, piece(0), far.at[s, k], off, unit)
+            self.base = piece(0)
+
+        def spread(self, p):
+            s, unit, axis, piece = self.s, UNITS_OF[p], self.order[p], self.pieces[p]
+            if p == 2:
+                self.finish(2)
+                pay[ds(mine + self.base, unit), :] = work[ds(self.base, unit), :]
+            else:
+                self.last.wait_recv()
+                if self.last2 is not None:
+                    self.last2.wait_recv()
+            own = pay.at[ds(mine + piece(0), unit)]
+            self.u = remote(own, own, ag_sem.at[s, p, 0], device(axis, 1))
+            self.d = remote(own, own, ag_sem.at[s, p, 1], device(axis, -1))
+            if p == 0:
+                self.ends = [remote(own, own, end_sem.at[s, 0], twin)]
+
+        def relay(self, p):
+            s, unit, axis, piece = self.s, UNITS_OF[p], self.order[p], self.pieces[p]
+            left, right = halves(unit)
+            self.u.wait_recv()
+            part = pay.at[ds(mine + piece(-1), left)]
+            self.last = remote(part, part, ag_sem.at[s, p, 2], device(axis, 1))
+            self.d.wait_recv()
+            self.last2 = None
+            if right:
+                part = pay.at[ds(mine + piece(1) + left, right)]
+                self.last2 = remote(part, part, ag_sem.at[s, p, 3], device(axis, -1))
+            if p == 0:
+                for k, i in ((1, -1), (2, 1)):
+                    part = pay.at[ds(mine + piece(i), unit)]
+                    self.ends.append(remote(part, part, end_sem.at[s, k], twin))
+
+        def tail(self):
+            self.last.wait_recv()
+            if self.last2 is not None:
+                self.last2.wait_recv()
+            part = pay.at[ds(mine + self.pieces[0](2), UNITS_OF[0])]
+            self.ends.append(remote(part, part, end_sem.at[self.s, 3], twin))
+
+        def end(self):
+            for copy in self.ends:
+                copy.wait_recv()
+
+        def run(self, stage):
+            if stage < 6:
+                (self.sides if stage % 2 else self.opposite)(stage // 2)
+            elif stage < 12:
+                (self.relay if stage % 2 else self.spread)(2 - (stage - 6) // 2)
+            elif stage == 12:
+                self.tail()
+            elif stage == 13:
+                self.end()
+
+    streams = [Stream(s) for s in range(STREAMS)]
+    per = PART // SB
+    for t in range(14 + ROUNDS - 1):
+        if t < ROUNDS:
+            for s in range(3 * t, 3 * t + 3):
+                for k in range(per):
+                    gram(1 - core, s * per + k, outbox)
+                if s == 0:
+                    pl.semaphore_wait(barrier, 7)
+                streams[s].swap()
+            for s in range(3 * t, 3 * t + 3):
+                for k in range(per):
+                    gram(core, s * per + k, work)
+        for r in range(ROUNDS):
+            if 0 <= t - r < 14:
+                for c in range(3):
+                    streams[3 * r + c].run(t - r)
+    for copy in started:
         copy.wait_send()
 
 
-def reduce_call(payload):
-    units = CHUNK // 4 + CHUNK // 16 + CHUNK // 64
+def reduce_call(blocks, coefficients, residuals, scale):
+    obs = blocks.shape[0]
+    units = sum(UNITS_OF)
     return pl.pallas_call(
-        reduce_kernel,
+        functools.partial(reduce_kernel, scale),
         out_shape=jax.ShapeDtypeStruct((ROWS, SB), F32),
-        in_specs=[pl.BlockSpec(memory_space=pltpu.VMEM)],
+        in_specs=[pl.BlockSpec(memory_space=pltpu.VMEM)] * 3,
         out_specs=pl.BlockSpec(memory_space=pltpu.VMEM),
         scratch_shapes=[
+            pltpu.VMEM((obs, G), BF16),
+            pltpu.VMEM((G, obs), BF16),
             pltpu.VMEM((HALF, SB), F32),
-            pltpu.VMEM((3, units, SB), F32),
-            pltpu.VMEM((3, 2, units, SB), F32),
-            pltpu.SemaphoreType.DMA((3, 2)),
-            pltpu.SemaphoreType.DMA((3, 3, 4, 2)),
-            pltpu.SemaphoreType.DMA((3, 3, 4, 2)),
-            pltpu.SemaphoreType.DMA((3, 2)),
+            pltpu.VMEM((HALF, SB), F32),
+            pltpu.VMEM((HALF, SB), F32),
+            pltpu.VMEM((STREAMS, units, SB), F32),
+            pltpu.VMEM((STREAMS, 2, units, SB), F32),
+            pltpu.SemaphoreType.DMA((STREAMS, 2)),
+            pltpu.SemaphoreType.DMA((STREAMS, 3, 4, 2)),
+            pltpu.SemaphoreType.DMA((STREAMS, 3, 4, 2)),
+            pltpu.SemaphoreType.DMA((STREAMS, 4, 2)),
         ],
         compiler_params=pltpu.CompilerParams(
             vmem_limit_bytes=60 * 1024 * 1024, collective_id=0, has_side_effects=True
         ),
         name="reduce",
-    )(payload)
-
-
-def split(x):
-    hi = x.astype(BF16)
-    return hi, (x - hi.astype(F32)).astype(BF16)
-
-
-def dot_nt(a, b):
-    return lax.dot_general(a, b, (((1,), (1,)), ((), ())), preferred_element_type=F32)
-
-
-def dot_nn(a, b):
-    return lax.dot_general(a, b, (((1,), (0,)), ((), ())), preferred_element_type=F32)
-
-
-def lane_all(x, lane):
-    return jnp.broadcast_to(x[:, lane : lane + 1], x.shape)
-
-
-def row_all(x, row):
-    return jnp.broadcast_to(x[row : row + 1, :], x.shape)
+    )(blocks, coefficients.reshape(obs, -1), residuals.reshape(1, obs))
 
 
 NEAR = 3
@@ -521,8 +553,7 @@
 
 
 def on_device(total, blocks, coefficients, residuals):
-    payload = gram_call(blocks, coefficients, residuals, 1.0 / total)
-    payload = reduce_call(payload)
+    payload = reduce_call(blocks, coefficients, residuals, 1.0 / total)
     pos = jnp.stack([lax.axis_index("gx"), lax.axis_index("gy")]).astype(jnp.int32)
     factor, answer = cholesky_call(pos, payload)
     return factor.reshape(1, 2, BS, 1, 2, BS), answer[0].reshape(G // BS, BS)

time: 212 us -> 180 us (0.85)
  Pallas kernels: 203 us -> 171 us
    pallas_call x2 -> x1, Pallas kernels: 115 us -> 82.7 us  [reduce_call(): pl.pallas_call(functools.partial(reduce_kernel, scale), out_shape=jax.Sha...]
where the time goes in v3:
time: 180 us; the launch traced here: 179 us
  Pallas kernels  171 us (95%)
  local copies, waits for them, and re-layouts  7.37 us (4%)
    pallas_call x1, Pallas kernels, cholesky_call(): pl.pallas_call(chol_kernel, out_shape=(jax.ShapeDtypeStruct((2, BS, 2 * B...  88 us
    pallas_call x1, Pallas kernels, reduce_call(): pl.pallas_call(functools.partial(reduce_kernel, scale), out_shape=jax.Sha...  82.7 us
    unnamed x2, local copies, waits for them, and re-layouts  4.15 us

profile of v3, /device:TPU:1, one launch (start us, length us, event | category | flops | bytes accessed | tf_op | source)
XLA Modules:
  0.0 179.4 jit_solution(3398548102561008304)
XLA Ops:
  0.6 0.6 pad_add_fusion.pos_ref
  1.2 1.8 copy.6.blk_ref
  3.0 2.4 %copy.10 = bf16[128,8,4,128]{3,1,2,0:T(8,128)(2,1)} copy(bf16[128,8,4,128]{3,2,1,0:T(4,128)(2,1)} %bitcast.10) | data formatting | bytes 2097152
  5.4 82.7 %reduce.1.mat_ref = f32[9216,256]{1,0:T(8,128)} custom-call(s32[1024,4]{1,0:T(8,128)} %copy.6.blk_ref, bf16[1024,512]{1,0:T(8,128)(2,1)} %bitcast.9, f32[1,1024]{1,0:T(1,128)} %bitcast.13), custom_call_target="tpu_custom_call" | custom-call | tf_op jit(solution)/shard_map/reduce/pallas_call | solution.py:267
  88.1 88.0 %chol.1 = (f32[2,128,256]{2,1,0:T(8,128)}, f32[8,2048]{1,0:T(8,128)}) custom-call(s32[2]{0:T(128)} %pad_add_fusion.pos_ref, s32[16,35]{1,0:T(8,128)} %constant.12.clone.plan_ref, f32[9216,256]{1,0:T(8,128)} %reduce.1.mat_ref), custom_call_target="tpu_custom_call" | custom-call | tf_op jit(solution)/shard_map/chol/pallas_call | solution.py:532
  176.1 1.8 reshape.15
  177.9 1.4 slice.3

commit v4 on v3

v4 whole, which is shorter than its diff:
```python
import functools

import jax
import jax.numpy as jnp
from jax import lax
from jax.experimental import pallas as pl
from jax.experimental.pallas import tpu as pltpu
from jax.sharding import PartitionSpec as P

G = 2048
BS = 128
SB = 2 * BS
NS = G // SB
EXTRA = 16
F32 = jnp.float32
BF16 = jnp.bfloat16
MESH = pl.DeviceIdType.MESH
ROUNDS = 3
SKEW = 1
STAGES = 10
STREAMS = 3 * ROUNDS
DIAG = [(j, j) for j in range(NS)]
SIDE = [(i, j) for j in range(NS) for i in range(j + 1, NS)]
TILES = DIAG[0::2] + SIDE[0::2] + DIAG[1::2] + SIDE[1::2]
ROWS = len(TILES) * SB
HALF = ROWS // 2
PART = HALF // STREAMS
UNITS_OF = (PART // 4, PART // 16, PART // 64)
ORDERS = ("xyz", "yzx", "zxy")


def split(x):
    hi = x.astype(BF16)
    return hi, (x - hi.astype(F32)).astype(BF16)


def dot_nt(a, b):
    return lax.dot_general(a, b, (((1,), (1,)), ((), ())), preferred_element_type=F32)


def dot_nn(a, b):
    return lax.dot_general(a, b, (((1,), (0,)), ((), ())), preferred_element_type=F32)


def lane_all(x, lane):
    return jnp.broadcast_to(x[:, lane : lane + 1], x.shape)


def row_all(x, row):
    return jnp.broadcast_to(x[row : row + 1, :], x.shape)


def place_of(x, y, z, core):
    return (lax.rem(y, 2) * 4 + x, z * 2 + core, y // 2)


def reduce_kernel(scale, blk_ref, coef_ref, res_ref, pay, design, flipped, outbox, inbox, work, near, far, swap_sem, rs_sem, ag_sem, end_sem):
    gx, gy, gz = lax.axis_index("gx"), lax.axis_index("gy"), lax.axis_index("gz")
    at = {"x": lax.rem(gx, 4), "y": gz * 2 + gx // 4, "z": gy // 2}
    core = lax.rem(gy, 2)

    def device(axis, shift):
        c = dict(at)
        c[axis] = lax.rem(c[axis] + shift + 4, 4)
        return place_of(c["x"], c["y"], c["z"], core)

    twin = place_of(at["x"], at["y"], at["z"], 1 - core)
    barrier = pltpu.get_barrier_semaphore()
    for axis in "xyz":
        for shift in (1, 2, 3):
            pl.semaphore_signal(barrier, inc=1, device_id=device(axis, shift), device_id_type=MESH)
    pl.semaphore_signal(barrier, inc=1, device_id=twin, device_id_type=MESH)

    obs = blk_ref.shape[0]
    slots = blk_ref.shape[1]
    step = 256

    def place(t, c):
        rows = pl.ds(pl.multiple_of(t * step, step), step)
        ids = [jnp.broadcast_to(blk_ref[rows, s : s + 1], (step, BS)) for s in range(slots)]
        vals = [coef_ref[rows, s * BS : (s + 1) * BS].astype(F32) for s in range(slots)]
        for b in range(G // BS):
            d = jnp.zeros((step, BS), F32)
            for s in range(slots):
                d = jnp.where(ids[s] == b, vals[s], d)
            db = d.astype(BF16)
            design[rows, b * BS : (b + 1) * BS] = db
            flipped[b * BS : (b + 1) * BS, rows] = db.T
        return c

    lax.fori_loop(0, obs // step, place, 0)

    res = res_ref[...]
    r1 = res.astype(BF16).astype(F32)
    r2 = (res - r1).astype(BF16).astype(F32)
    r3 = res - r1 - r2
    first = lax.broadcasted_iota(jnp.int32, (8, obs), 0)
    lhs = jnp.where(first == 0, r1, jnp.where(first == 1, r2, jnp.where(first == 2, r3, 0.0))).astype(BF16)

    def ds(start, size):
        return pl.ds(pl.multiple_of(start, 8), size)

    mine = core * HALF

    def gram(side, slot, dst, plus=None):
        (i0, j0), (i1, j1) = TILES[slot], TILES[slot + len(TILES) // 2]
        i = (i0 + (i1 - i0) * side) * SB
        j = (j0 + (j1 - j0) * side) * SB
        cols = design[:, pl.ds(pl.multiple_of(j, SB), SB)]
        base = slot * SB
        tile = dot_nn(flipped[pl.ds(pl.multiple_of(i, SB), SB), :], cols) * scale
        dst[base : base + SB, :] = tile if plus is None else tile + plus[base : base + SB, :]
        if i0 == j0:
            row = jnp.sum(dot_nn(lhs, cols), axis=0, keepdims=True) * scale
            rows = jnp.concatenate([row[:, :BS], row[:, BS:], jnp.zeros((6, BS), F32)], axis=0)
            dst[base : base + 8, BS:] = rows if plus is None else rows + plus[base : base + 8, BS:]

    started = []

    def remote(src, dst, sems, to):
        copy = pltpu.make_async_remote_copy(
            src_ref=src, dst_ref=dst, send_sem=sems.at[0], recv_sem=sems.at[1], device_id=to, device_id_type=MESH
        )
        copy.start()
        started.append(copy)
        return copy

    def add(dst, dst_start, srcs, src_start, size, goal=None):
        piece = min(size, 64)
        goal, goal_start = (dst, dst_start) if goal is None else goal

        def body(t, carry):
            total = dst[ds(dst_start + t * piece, piece), :]
            for src in srcs:
                total = total + src[ds(src_start + t * piece, piece), :]
            goal[ds(goal_start + t * piece, piece), :] = total
            return carry

        if size == piece:
            body(0, 0)
        else:
            lax.fori_loop(0, size // piece, body, 0)

    class Stream:
        def __init__(self, s):
            self.s = s
            self.order = ORDERS[s % 3]
            self.base = s * PART
            self.pieces = []

        def swap(self):
            rows = PART * self.s
            self.swapped = remote(outbox.at[ds(rows, PART)], inbox.at[ds(rows, PART)], swap_sem.at[self.s], twin)

        def opposite(self):
            s, unit = self.s, UNITS_OF[0]
            piece, axis = self.enter(0), self.order[0]
            half = unit // 2
            self.a = remote(work.at[ds(piece(2), half)], near.at[s, ds(0, half)], rs_sem.at[s, 0, 0], device(axis, 1))
            self.b = remote(
                work.at[ds(piece(2) + half, half)], near.at[s, ds(half, half)], rs_sem.at[s, 0, 1], device(axis, -1)
            )

        def enter(self, p):
            m, base, unit = at[self.order[p]], self.base, UNITS_OF[p]
            self.pieces.append(lambda i: base + lax.rem(m + i + 4, 4) * unit)
            return self.pieces[p]

        def sides(self):
            s, unit, axis, piece = self.s, UNITS_OF[0], self.order[0], self.pieces[0]
            half = unit // 2
            self.a.wait_recv()
            add(work, piece(1), (near.at[s],), 0, half)
            u = remote(work.at[ds(piece(1), unit)], far.at[s, 0, ds(0, unit)], rs_sem.at[s, 0, 2], device(axis, 1))
            self.b.wait_recv()
            add(work, piece(-1) + half, (near.at[s],), half, half)
            d = remote(work.at[ds(piece(-1), unit)], far.at[s, 1, ds(0, unit)], rs_sem.at[s, 0, 3], device(axis, -1))
            self.wait = (u, d)

        def finish(self, p):
            for copy in self.wait:
                copy.wait_recv()
            self.base = self.pieces[p](0)
            goal = (pay, mine + self.base) if p == 2 else None
            srcs = tuple(far.at[self.s, k] for k in range(len(self.wait)))
            add(work, self.base, srcs, sum(UNITS_OF[:p]), UNITS_OF[p], goal)

        def exchange(self, p):
            self.finish(p - 1)
            s, unit, piece, axis = self.s, UNITS_OF[p], self.enter(p), self.order[p]
            off = sum(UNITS_OF[:p])
            self.wait = tuple(
                remote(work.at[ds(piece(i), unit)], far.at[s, i - 1, ds(off, unit)], rs_sem.at[s, p, i - 1], device(axis, i))
                for i in (1, 2, 3)
            )

        def spread(self, p):
            s, unit, axis, piece = self.s, UNITS_OF[p], self.order[p], self.pieces[p]
            if p == 2:
                self.finish(2)
            else:
                for copy in self.wait:
                    copy.wait_recv()
            own = pay.at[ds(mine + piece(0), unit)]
            shifts = (1, 2, 3) if p else (1, 3)
            self.wait = tuple(remote(own, own, ag_sem.at[s, p, i - 1], device(axis, i)) for i in shifts)
            if p == 0:
                self.ends = [remote(own, own, end_sem.at[s, 0], twin)]

        def relay(self):
            s, unit, axis, piece = self.s, UNITS_OF[0], self.order[0], self.pieces[0]
            half = unit // 2
            u, d = self.wait
            u.wait_recv()
            part = pay.at[ds(mine + piece(-1), half)]
            up = remote(part, part, ag_sem.at[s, 0, 1], device(axis, 1))
            d.wait_recv()
            part = pay.at[ds(mine + piece(1) + half, half)]
            down = remote(part, part, ag_sem.at[s, 0, 3], device(axis, -1))
            self.wait = (up, down)
            for k, i in ((1, -1), (2, 1)):
                part = pay.at[ds(mine + piece(i), unit)]
                self.ends.append(remote(part, part, end_sem.at[s, k], twin))

        def tail(self):
            for copy in self.wait:
                copy.wait_recv()
            part = pay.at[ds(mine + self.pieces[0](2), UNITS_OF[0])]
            self.ends.append(remote(part, part, end_sem.at[self.s, 3], twin))

        def end(self):
            for copy in self.ends:
                copy.wait_recv()

        def run(self, stage):
            if stage == 0:
                self.opposite()
            elif stage == 1:
                self.sides()
            elif stage < 4:
                self.exchange(stage - 1)
            elif stage < 7:
                self.spread(6 - stage)
            elif stage == 7:
                self.relay()
            elif stage == 8:
                self.tail()
            else:
                self.end()

    streams = [Stream(s) for s in range(STREAMS)]
    per = PART // SB

    def give(r):
        for s in range(3 * r, 3 * r + 3):
            for k in range(per):
                gram(1 - core, s * per + k, outbox)
            if s == 0:
                pl.semaphore_wait(barrier, 10)
            streams[s].swap()

    def keep(r):
        for s in range(3 * r, 3 * r + 3):
            streams[s].swapped.wait_recv()
            for k in range(per):
                gram(core, s * per + k, work, inbox)
            streams[s].run(0)

    give(0)
    for t in range(STAGES + SKEW * (ROUNDS - 1)):
        for r in reversed(range(ROUNDS)):
            stage = t - SKEW * r
            if stage == 0:
                if r + 1 < ROUNDS:
                    give(r + 1)
                keep(r)
            elif 0 < stage < STAGES:
                for c in range(3):
                    streams[3 * r + c].run(stage)
    for copy in started:
        copy.wait_send()


def reduce_call(blocks, coefficients, residuals, scale):
    obs = blocks.shape[0]
    units = sum(UNITS_OF)
    return pl.pallas_call(
        functools.partial(reduce_kernel, scale),
        out_shape=jax.ShapeDtypeStruct((ROWS, SB), F32),
        in_specs=[pl.BlockSpec(memory_space=pltpu.VMEM)] * 3,
        out_specs=pl.BlockSpec(memory_space=pltpu.VMEM),
        scratch_shapes=[
            pltpu.VMEM((obs, G), BF16),
            pltpu.VMEM((G, obs), BF16),
            pltpu.VMEM((HALF, SB), F32),
            pltpu.VMEM((HALF, SB), F32),
            pltpu.VMEM((HALF, SB), F32),
            pltpu.VMEM((STREAMS, UNITS_OF[0], SB), F32),
            pltpu.VMEM((STREAMS, 3, units, SB), F32),
            pltpu.SemaphoreType.DMA((STREAMS, 2)),
            pltpu.SemaphoreType.DMA((STREAMS, 3, 4, 2)),
            pltpu.SemaphoreType.DMA((STREAMS, 3, 4, 2)),
            pltpu.SemaphoreType.DMA((STREAMS, 4, 2)),
        ],
        compiler_params=pltpu.CompilerParams(
            vmem_limit_bytes=60 * 1024 * 1024, collective_id=0, has_side_effects=True
        ),
        name="reduce",
    )(blocks, coefficients.reshape(obs, -1), residuals.reshape(1, obs))


SPLITS = (6, 12, 16)
DUMMY = G + EXTRA
TALL = DUMMY + SB + EXTRA
UNITS = 7
SOLVES = 2
LAG = 2
FIRST_UNIT = 6
SIDES = NS - 1


def plan():
    n = 2 * NS
    sides = [[DUMMY] * SIDES for _ in range(n)]
    units = [[(DUMMY, 0, 0, 0)] * UNITS for _ in range(n)]
    todo = []
    for k in range(n):
        if k:
            first = (k - 1) // 2 + (1 if k % 2 else 2)
            for t, i in enumerate(range(first, NS)):
                sides[k][t] = i * SB
        if k >= 2 and k % 2 == 0:
            p = k // 2 - 1
            for j in range(p + 1, NS):
                for i in range(j, NS):
                    if (i, j) != (p + 1, p + 1):
                        todo.append((2 * j if i > j else 2 * j - 1, j, p, i))
        todo.sort()
        now, todo = todo[:UNITS], todo[UNITS:]
        for t, (limit, j, p, i) in enumerate(now):
            assert limit >= k
            units[k][t] = (i * SB, j * SB, p * SB, 1 if i == j else 0)
    assert not todo
    flat = []
    for k in range(n):
        flat.append(sides[k] + [v for u in units[k] for v in u])
    return flat


def eliminate(w, fill):
    lane = lax.broadcasted_iota(jnp.int32, (8, BS), 1)
    sub = lax.broadcasted_iota(jnp.int32, (8, BS), 0)
    w = list(w)
    count = len(w)
    start = 0
    for g in range(count):
        end = min(e for e in SPLITS if e > g)
        if g == start:
            cols = [lane_all(w[g], 8 * g + j) for j in range(8)]
        r = w[g]
        group = (lane >= 8 * g) & (lane < 8 * g + 8)
        near = range(g + 1, end)
        raw = {i: [lane_all(w[i], 8 * g + j) for j in range(8)] for i in near}
        ahead = [lane_all(w[g + 1], 8 * g + 8 + j) for j in range(8)] if g + 1 < end else None
        accs = {i: jnp.where(group, 0.0, w[i]) for i in near}
        pivot = row_all(cols[0], 0)
        for j in range(8):
            root = lax.rsqrt(pivot)
            if j < 7:
                pivot = row_all(cols[j + 1], j + 1) - (row_all(cols[j], j + 1) * root) * (row_all(cols[j + 1], j) * root)
            scaled = cols[j] * root
            below = jnp.where(sub > j, scaled, 0.0)
            here = lane == 8 * g + j
            row = row_all(jnp.where(here, 1.0, r), j) * root
            r = jnp.where(sub == j, row, jnp.where(here & (sub > j), 0.0, r) - below * row)
            ups = {}
            for l in range(j + 1, 8):
                ups[l] = row_all(cols[l], j) * root
                cols[l] = cols[l] - scaled * ups[l]
            inverse_row = jnp.where((lane > 8 * g + j) & (lane < 8 * g + 8), 0.0, row)
            for i in near:
                c = raw[i]
                m = c[j] * root
                for l in range(j + 1, 8):
                    c[l] = c[l] - m * ups[l]
                accs[i] = accs[i] - m * inverse_row
                if i == g + 1:
                    ahead = [ahead[l] - m * row_all(m, l) for l in range(8)]
        w[g] = r
        for i in near:
            w[i] = accs[i]
        if g + 1 == end and end < count:
            xs, ys = [], []
            for i in range(start, end):
                xs.append(jnp.where(lane >= 8 * end, w[i], 0.0))
                ys.append(jnp.where((lane < 8 * end) & (lane > 8 * i + sub), 0.0, w[i]))
            xh, xl = split(jnp.concatenate(xs, axis=0))
            yh, yl = split(jnp.concatenate(ys, axis=0))
            delta = lax.dot_general(
                jnp.concatenate([xh, xl, xh], axis=0),
                jnp.concatenate([yh, yh, yl], axis=0),
                (((0,), (0,)), ((), ())),
                preferred_element_type=F32,
            )
            done = (lane >= 8 * start) & (lane < 8 * end)
            for i in range(end, count):
                w[i] = jnp.where(done, 0.0, w[i]) - delta[8 * i : 8 * i + 8]
            start = end
        cols = ahead
        fill(g)
    return w


def aligned(x, m=16):
    return pl.multiple_of(x, m)


def stacked(hi, lo):
    return jnp.concatenate(
        [jnp.concatenate([hi, hi], axis=1), jnp.concatenate([lo, jnp.zeros_like(lo)], axis=1)], axis=0
    )


def fold(o):
    return o[:, :BS] + o[:, BS:]


def chol_kernel(plan_ref, mat_ref, out_ref, sol_ref, a_ref, hi_ref, lo_ref, inv_ref, winv_ref, wnext_ref, y_ref, sem):
    n = G // BS
    copies = []
    for t, (i, j) in enumerate(TILES):
        copies.append(
            pltpu.make_async_copy(
                mat_ref.at[pl.ds(t * SB, SB)], a_ref.at[pl.ds(i * SB, SB), pl.ds(j * SB, SB)], sem.at[t]
            )
        )
        copies[-1].start()
    a_ref[pl.ds(G, EXTRA), :] = jnp.zeros((EXTRA, G), F32)
    for copy in copies:
        copy.wait()
    for j in range(NS):
        for h in range(2):
            a_ref[G : G + 1, j * SB + h * BS : j * SB + (h + 1) * BS] = a_ref[
                j * SB + h : j * SB + h + 1, j * SB + BS : (j + 1) * SB
            ]
    lane2 = lax.broadcasted_iota(jnp.int32, (BS, BS), 1)
    sub2 = lax.broadcasted_iota(jnp.int32, (BS, BS), 0)
    ext = pl.ds(G, EXTRA)

    def put(rows, cols, o):
        oh, ol = split(o)
        hi_ref[rows, cols] = oh
        lo_ref[rows, cols] = ol
        return jnp.concatenate([oh, ol], axis=1)

    def solved(rows_list, cols):
        x = jnp.concatenate([a_ref[rows, cols] for rows in rows_list], axis=0)
        xh, xl = split(x)
        return fold(dot_nt(jnp.concatenate([xh, xl], axis=1), winv_ref[...]))

    def update(rows, erows, jc, pc):
        xh = jnp.concatenate([hi_ref[rows, pc], hi_ref[ext, pc]], axis=0)
        xl = jnp.concatenate([lo_ref[rows, pc], lo_ref[ext, pc]], axis=0)
        rh, rl = hi_ref[jc, pc], lo_ref[jc, pc]
        o = dot_nt(xh, rh) + dot_nt(xl, rh) + dot_nt(xh, rl)
        a_ref[rows, jc] = a_ref[rows, jc] - o[:SB]
        a_ref[erows, jc] = a_ref[erows, jc] - o[SB:]

    def step(k, carry):
        at = aligned(k * BS, BS)
        cols = pl.ds(at, BS)
        odd = lax.rem(k, 2)
        prev = pl.ds(aligned(jnp.maximum(k - 1, 0) * BS, BS), BS)
        edummy = DUMMY + SB
        eside = pl.ds(aligned(jnp.where(odd == 1, G, edummy)), EXTRA)

        waiting = {}

        def solve_side(t):
            rows = pl.ds(aligned(plan_ref[k, t]), SB)
            o = solved([rows, eside] if t == 0 else [rows], prev)
            both = put(rows, prev, o[:SB])
            if t == 0:
                both = jnp.concatenate([both, put(eside, prev, o[SB:])], axis=0)
            waiting[t] = both

        def update_side(t):
            d = fold(dot_nt(waiting.pop(t), wnext_ref[...]))
            rows = pl.ds(aligned(jnp.where(odd == 1, plan_ref[k, t], DUMMY)), SB)
            a_ref[rows, cols] = a_ref[rows, cols] - d[:SB]
            if t == 0:
                a_ref[eside, cols] = a_ref[eside, cols] - d[SB:]

        def tile_update(t):
            u = SIDES + 4 * t
            rows = pl.ds(aligned(plan_ref[k, u]), SB)
            jc = pl.ds(aligned(plan_ref[k, u + 1], SB), SB)
            pc = pl.ds(aligned(plan_ref[k, u + 2], SB), SB)
            update(rows, pl.ds(aligned(jnp.where(plan_ref[k, u + 3] == 1, G, edummy)), EXTRA), jc, pc)

        def fill(g):
            for t in range(SIDES):
                if t // SOLVES == g:
                    solve_side(t)
            for t in range(SIDES):
                if t // SOLVES + LAG == g:
                    update_side(t)
            if FIRST_UNIT <= g < FIRST_UNIT + UNITS:
                tile_update(g - FIRST_UNIT)

        block = a_ref[pl.ds(at, BS), cols]
        w = eliminate([block[8 * i : 8 * i + 8] for i in range(BS // 8)], fill)
        w = jnp.concatenate(w, axis=0)
        inv = jnp.where(lane2 <= sub2, w, 0.0)
        inv_ref[pl.ds(at, BS), :] = inv
        ih, il = split(inv)
        winv_ref[...] = stacked(ih, il)

        @pl.when(odd == 0)
        def _():
            nxt = pl.ds(aligned(at + BS, BS), BS)
            o = solved([nxt], cols)
            both = put(nxt, cols, o)
            weights = stacked(both[:, :BS], both[:, BS:])
            wnext_ref[...] = weights
            a_ref[nxt, nxt] = a_ref[nxt, nxt] - fold(dot_nt(both, weights))

        @pl.when((odd == 1) & (k < n - 1))
        def _():
            nxt = pl.ds(aligned(at + BS, BS), SB)
            o = solved([nxt, ext], cols)
            put(nxt, cols, o[:SB])
            put(ext, cols, o[SB:])
            update(nxt, ext, nxt, pl.ds(aligned(at - BS, SB), SB))

        @pl.when(k == n - 1)
        def _():
            put(ext, cols, solved([ext], cols))

        a_ref[pl.ds(at, BS), cols] = jnp.where(lane2 == sub2, 1.0 / w, jnp.where(lane2 > sub2, w, 0.0)).T
        return carry

    lax.fori_loop(0, n, step, 0)

    def back(s, c):
        k = n - 1 - s
        at = aligned(k * BS, BS)
        cols = pl.ds(at, BS)
        ih, il = split(inv_ref[pl.ds(at, BS), :])
        yh, yl = split(y_ref[:, cols])
        y = jnp.concatenate([yh, yl], axis=0)
        z = dot_nn(y, ih)
        z = z[:8] + z[8:] + dot_nn(yh, il)
        sol_ref[pl.ds(k, 1), :] = z[:1]
        zh, zl = split(z)
        zz = jnp.concatenate([zh, zl], axis=0)
        wide = 4 * BS

        def sub(j, c2):
            jc = pl.ds(aligned(j * wide, wide), wide)
            o = dot_nn(zz, hi_ref[pl.ds(at, BS), jc])
            y_ref[:, jc] = y_ref[:, jc] - (o[:8] + o[8:] + dot_nn(zh, lo_ref[pl.ds(at, BS), jc]))
            return c2

        lax.fori_loop(0, (k + 3) // 4, sub, 0)
        return c

    y_ref[...] = hi_ref[ext, :].astype(F32)[:8] + lo_ref[ext, :].astype(F32)[:8]
    lax.fori_loop(0, n, back, 0)

    p, q = lax.axis_index("gx"), lax.axis_index("gy")
    for r in range(2):
        for c in range(2):
            rb = r * 8 + p
            cb = c * 8 + q
            rows = pl.ds(aligned(rb * BS, BS), BS)
            cols = pl.ds(aligned(cb * BS, BS), BS)
            off = hi_ref[rows, cols].astype(F32) + lo_ref[rows, cols].astype(F32)
            out_ref[r, :, c, :] = jnp.where(rb > cb, off, jnp.where(rb == cb, a_ref[rows, cols], 0.0))


def cholesky_call(payload):
    return pl.pallas_call(
        chol_kernel,
        out_shape=(jax.ShapeDtypeStruct((2, BS, 2, BS), F32), jax.ShapeDtypeStruct((G // BS, BS), F32)),
        in_specs=[
            pl.BlockSpec(memory_space=pltpu.SMEM),
            pl.BlockSpec(memory_space=pl.ANY),
        ],
        out_specs=(pl.BlockSpec(memory_space=pltpu.VMEM), pl.BlockSpec(memory_space=pltpu.VMEM)),
        scratch_shapes=[
            pltpu.VMEM((TALL, G), F32),
            pltpu.VMEM((TALL, G), BF16),
            pltpu.VMEM((TALL, G), BF16),
            pltpu.VMEM((G, BS), F32),
            pltpu.VMEM((SB, SB), BF16),
            pltpu.VMEM((SB, SB), BF16),
            pltpu.VMEM((8, G), F32),
            pltpu.SemaphoreType.DMA((len(TILES),)),
        ],
        compiler_params=pltpu.CompilerParams(vmem_limit_bytes=60 * 1024 * 1024),
        name="chol",
    )(jnp.asarray(plan(), jnp.int32), payload)


def on_device(total, blocks, coefficients, residuals):
    payload = reduce_call(blocks, coefficients, residuals, 1.0 / total)
    factor, answer = cholesky_call(payload)
    return factor.reshape(1, 2, BS, 1, 2, BS), answer


def solution(mesh):
    def whole(blocks, coefficients, residuals):
        spread = P(("gx", "gy", "gz"))
        return jax.shard_map(
            functools.partial(on_device, blocks.shape[0]),
            mesh=mesh,
            in_specs=(spread, spread, spread),
            out_specs=(P("gx", None, None, "gy", None, None), P()),
            check_vma=False,
        )(blocks, coefficients, residuals)

    return whole
```

time: 180 us -> 150 us (0.83)
  Pallas kernels: 171 us -> 145 us
  local copies, waits for them, and re-layouts: 7.37 us -> 4.15 us
    pallas_call x1, Pallas kernels: 88 us -> 74.1 us  [cholesky_call(): pl.pallas_call(chol_kernel, out_shape=(jax.ShapeDtypeStruct((2, BS, 2, BS...]
    pallas_call x1, Pallas kernels: 82.7 us -> 70.7 us  [reduce_call(): pl.pallas_call(functools.partial(reduce_kernel, scale), out_shape=jax.Sha...]
where the time goes in v4:
time: 150 us
  Pallas kernels  145 us (97%)
  local copies, waits for them, and re-layouts  4.15 us (3%)
    pallas_call x1, Pallas kernels, cholesky_call(): pl.pallas_call(chol_kernel, out_shape=(jax.ShapeDtypeStruct((2, BS, 2, BS...  74.1 us
    pallas_call x1, Pallas kernels, reduce_call(): pl.pallas_call(functools.partial(reduce_kernel, scale), out_shape=jax.Sha...  70.7 us
    unnamed x2, local copies, waits for them, and re-layouts  4.15 us

profile of v4, /device:TPU:1, one launch (start us, length us, event | category | flops | bytes accessed | tf_op | source)
XLA Modules:
  0.0 149.8 jit_solution(6410607258476675403)
XLA Ops:
  0.6 1.8 %copy.6.blk_ref = s32[1024,4]{1,0:T(8,128)} copy(s32[1024,4]{0,1:T(4,128)} %param.4) | data formatting | bytes 32768 | tf_op args[0]
  2.4 2.4 %copy.10 = bf16[128,8,4,128]{3,1,2,0:T(8,128)(2,1)} copy(bf16[128,8,4,128]{3,2,1,0:T(4,128)(2,1)} %bitcast.9) | data formatting | bytes 2097152
  4.8 70.7 %reduce.1.mat_ref = f32[9216,256]{1,0:T(8,128)} custom-call(s32[1024,4]{1,0:T(8,128)} %copy.6.blk_ref, bf16[1024,512]{1,0:T(8,128)(2,1)} %bitcast.8, f32[1,1024]{1,0:T(1,128)} %bitcast.10), custom_call_target="tpu_custom_call" | custom-call | tf_op jit(solution)/shard_map/reduce/pallas_call | solution.py:287
  75.5 74.1 %chol.1 = (f32[2,128,2,128]{3,2,1,0:T(2,128)}, f32[16,128]{1,0:T(8,128)}) custom-call(s32[16,35]{1,0:T(8,128)} %constant.2.clone.plan_ref, f32[9216,256]{1,0:T(8,128)} %reduce.1.mat_ref), custom_call_target="tpu_custom_call" | custom-call | tf_op jit(solution)/shard_map/chol/pallas_call | solution.py:583

commit v5 on v4

--- a/solution.py
+++ b/solution.py
@@ -17,6 +17,8 @@
 MESH = pl.DeviceIdType.MESH
 ROUNDS = 3
 SKEW = 1
+RED_MB = 34
+CHOL_MB = 44
 STAGES = 10
 STREAMS = 3 * ROUNDS
 DIAG = [(j, j) for j in range(NS)]
@@ -71,13 +73,12 @@
             pl.semaphore_signal(barrier, inc=1, device_id=device(axis, shift), device_id_type=MESH)
     pl.semaphore_signal(barrier, inc=1, device_id=twin, device_id_type=MESH)
 
-    obs = blk_ref.shape[0]
-    slots = blk_ref.shape[1]
+    slots, obs = blk_ref.shape
     step = 256
 
     def place(t, c):
         rows = pl.ds(pl.multiple_of(t * step, step), step)
-        ids = [jnp.broadcast_to(blk_ref[rows, s : s + 1], (step, BS)) for s in range(slots)]
+        ids = [jnp.broadcast_to(blk_ref[s : s + 1, rows], (BS, step)).T for s in range(slots)]
         vals = [coef_ref[rows, s * BS : (s + 1) * BS].astype(F32) for s in range(slots)]
         for b in range(G // BS):
             d = jnp.zeros((step, BS), F32)
@@ -303,15 +304,16 @@
             pltpu.SemaphoreType.DMA((STREAMS, 4, 2)),
         ],
         compiler_params=pltpu.CompilerParams(
-            vmem_limit_bytes=60 * 1024 * 1024, collective_id=0, has_side_effects=True
+            vmem_limit_bytes=RED_MB * 1024 * 1024, collective_id=0, has_side_effects=True
         ),
         name="reduce",
-    )(blocks, coefficients.reshape(obs, -1), residuals.reshape(1, obs))
+    )(blocks.T, coefficients.reshape(obs, -1), residuals.reshape(1, obs))
 
 
 SPLITS = (6, 12, 16)
 DUMMY = G + EXTRA
 TALL = DUMMY + SB + EXTRA
+SEGMENTS = ((0, 8, 7, 7), (8, 14, 3, 6), (14, 16, 1, 0))
 UNITS = 7
 SOLVES = 2
 LAG = 2
@@ -336,7 +338,8 @@
                     if (i, j) != (p + 1, p + 1):
                         todo.append((2 * j if i > j else 2 * j - 1, j, p, i))
         todo.sort()
-        now, todo = todo[:UNITS], todo[UNITS:]
+        room = next(u for a, b, _, u in SEGMENTS if a <= k < b)
+        now, todo = todo[:room], todo[room:]
         for t, (limit, j, p, i) in enumerate(now):
             assert limit >= k
             units[k][t] = (i * SB, j * SB, p * SB, 1 if i == j else 0)
@@ -425,24 +428,15 @@
     return o[:, :BS] + o[:, BS:]
 
 
-def chol_kernel(plan_ref, mat_ref, out_ref, sol_ref, a_ref, hi_ref, lo_ref, inv_ref, winv_ref, wnext_ref, y_ref, sem):
+def chol_kernel(plan_ref, mat_ref, out_ref, sol_ref, a_ref, hi_ref, lo_ref, inv_ref, winv_ref, wnext_ref, y_ref):
     n = G // BS
-    copies = []
     for t, (i, j) in enumerate(TILES):
-        copies.append(
-            pltpu.make_async_copy(
-                mat_ref.at[pl.ds(t * SB, SB)], a_ref.at[pl.ds(i * SB, SB), pl.ds(j * SB, SB)], sem.at[t]
-            )
-        )
-        copies[-1].start()
+        a_ref[i * SB : (i + 1) * SB, j * SB : (j + 1) * SB] = mat_ref[t * SB : (t + 1) * SB, :]
     a_ref[pl.ds(G, EXTRA), :] = jnp.zeros((EXTRA, G), F32)
-    for copy in copies:
-        copy.wait()
     for j in range(NS):
+        t = TILES.index((j, j)) * SB
         for h in range(2):
-            a_ref[G : G + 1, j * SB + h * BS : j * SB + (h + 1) * BS] = a_ref[
-                j * SB + h : j * SB + h + 1, j * SB + BS : (j + 1) * SB
-            ]
+            a_ref[G : G + 1, j * SB + h * BS : j * SB + (h + 1) * BS] = mat_ref[t + h : t + h + 1, BS:]
     lane2 = lax.broadcasted_iota(jnp.int32, (BS, BS), 1)
     sub2 = lax.broadcasted_iota(jnp.int32, (BS, BS), 0)
     ext = pl.ds(G, EXTRA)
@@ -466,7 +460,7 @@
         a_ref[rows, jc] = a_ref[rows, jc] - o[:SB]
         a_ref[erows, jc] = a_ref[erows, jc] - o[SB:]
 
-    def step(k, carry):
+    def step(sides, count, k, carry):
         at = aligned(k * BS, BS)
         cols = pl.ds(at, BS)
         odd = lax.rem(k, 2)
@@ -499,13 +493,13 @@
             update(rows, pl.ds(aligned(jnp.where(plan_ref[k, u + 3] == 1, G, edummy)), EXTRA), jc, pc)
 
         def fill(g):
-            for t in range(SIDES):
+            for t in range(sides):
                 if t // SOLVES == g:
                     solve_side(t)
-            for t in range(SIDES):
+            for t in range(sides):
                 if t // SOLVES + LAG == g:
                     update_side(t)
-            if FIRST_UNIT <= g < FIRST_UNIT + UNITS:
+            if FIRST_UNIT <= g < FIRST_UNIT + count:
                 tile_update(g - FIRST_UNIT)
 
         block = a_ref[pl.ds(at, BS), cols]
@@ -540,29 +534,27 @@
         a_ref[pl.ds(at, BS), cols] = jnp.where(lane2 == sub2, 1.0 / w, jnp.where(lane2 > sub2, w, 0.0)).T
         return carry
 
-    lax.fori_loop(0, n, step, 0)
+    for first, last, sides, count in SEGMENTS:
+        lax.fori_loop(first, last, functools.partial(step, sides, count), 0)
+
+    def column(row):
+        return jnp.broadcast_to(row, (BS, BS)).T
 
     def back(s, c):
         k = n - 1 - s
         at = aligned(k * BS, BS)
         cols = pl.ds(at, BS)
-        ih, il = split(inv_ref[pl.ds(at, BS), :])
-        yh, yl = split(y_ref[:, cols])
-        y = jnp.concatenate([yh, yl], axis=0)
-        z = dot_nn(y, ih)
-        z = z[:8] + z[8:] + dot_nn(yh, il)
-        sol_ref[pl.ds(k, 1), :] = z[:1]
-        zh, zl = split(z)
-        zz = jnp.concatenate([zh, zl], axis=0)
-        wide = 4 * BS
+        z = jnp.sum(column(y_ref[0:1, cols]) * inv_ref[pl.ds(at, BS), :], axis=0, keepdims=True)
+        sol_ref[pl.ds(k, 1), :] = z
+        zc = column(z)
 
         def sub(j, c2):
-            jc = pl.ds(aligned(j * wide, wide), wide)
-            o = dot_nn(zz, hi_ref[pl.ds(at, BS), jc])
-            y_ref[:, jc] = y_ref[:, jc] - (o[:8] + o[8:] + dot_nn(zh, lo_ref[pl.ds(at, BS), jc]))
+            jc = pl.ds(aligned(j * SB, SB), SB)
+            block = hi_ref[pl.ds(at, BS), jc].astype(F32) + lo_ref[pl.ds(at, BS), jc].astype(F32)
+            y_ref[0:1, jc] = y_ref[0:1, jc] - jnp.sum(jnp.concatenate([zc, zc], axis=1) * block, axis=0, keepdims=True)
             return c2
 
-        lax.fori_loop(0, (k + 3) // 4, sub, 0)
+        lax.fori_loop(0, (k + 1) // 2, sub, 0)
         return c
 
     y_ref[...] = hi_ref[ext, :].astype(F32)[:8] + lo_ref[ext, :].astype(F32)[:8]
@@ -585,7 +577,7 @@
         out_shape=(jax.ShapeDtypeStruct((2, BS, 2, BS), F32), jax.ShapeDtypeStruct((G // BS, BS), F32)),
         in_specs=[
             pl.BlockSpec(memory_space=pltpu.SMEM),
-            pl.BlockSpec(memory_space=pl.ANY),
+            pl.BlockSpec(memory_space=pltpu.VMEM),
         ],
         out_specs=(pl.BlockSpec(memory_space=pltpu.VMEM), pl.BlockSpec(memory_space=pltpu.VMEM)),
         scratch_shapes=[
@@ -596,9 +588,8 @@
             pltpu.VMEM((SB, SB), BF16),
             pltpu.VMEM((SB, SB), BF16),
             pltpu.VMEM((8, G), F32),
-            pltpu.SemaphoreType.DMA((len(TILES),)),
         ],
-        compiler_params=pltpu.CompilerParams(vmem_limit_bytes=60 * 1024 * 1024),
+        compiler_params=pltpu.CompilerParams(vmem_limit_bytes=CHOL_MB * 1024 * 1024),
         name="chol",
     )(jnp.asarray(plan(), jnp.int32), payload)
 

time: 150 us -> 134 us (0.89)
  Pallas kernels: 145 us -> 131 us
    pallas_call x1, Pallas kernels: 74.1 us -> 65 us  [cholesky_call(): pl.pallas_call(chol_kernel, out_shape=(jax.ShapeDtypeStruct((2, BS, 2, BS...]
    pallas_call x1, Pallas kernels: 70.7 us -> 65.7 us  [reduce_call(): pl.pallas_call(functools.partial(reduce_kernel, scale), out_shape=jax.Sha...]
    unnamed x2 -> x7, local copies, waits for them, and re-layouts: 4.15 us -> 2.82 us
where the time goes in v5:
time: 134 us
  Pallas kernels  131 us (98%)
  local copies, waits for them, and re-layouts  2.82 us (2%)
    pallas_call x1, Pallas kernels, reduce_call(): pl.pallas_call(functools.partial(reduce_kernel, scale), out_shape=jax.Sha...  65.7 us
    pallas_call x1, Pallas kernels, cholesky_call(): pl.pallas_call(chol_kernel, out_shape=(jax.ShapeDtypeStruct((2, BS, 2, BS...  65 us
    unnamed x7, local copies, waits for them, and re-layouts  2.82 us

profile of v5, /device:TPU:1, one launch (start us, length us, event | category | flops | bytes accessed | tf_op | source)
XLA Modules:
  0.0 134.2 jit_solution(2002284150697430405)
XLA Ops:
  0.6 0.0 copy-start.1
  0.6 1.4 %copy.9 = bf16[128,8,4,128]{3,1,2,0:T(8,128)(2,1)S(1)} copy(bf16[128,8,4,128]{3,2,1,0:T(4,128)(2,1)} %bitcast.12) | data formatting | bytes 2097152
  2.1 0.0 copy-start
  2.1 0.7 copy-done
  2.8 0.0 copy-start.2
  2.8 0.7 copy-done.2
  3.5 65.7 %reduce.1.mat_ref = f32[9216,256]{1,0:T(8,128)S(1)} custom-call(s32[4,1024]{1,0:T(4,128)S(1)} %bitcast.10, bf16[1024,512]{1,0:T(8,128)(2,1)S(1)} %bitcast.9, f32[1,1024]{1,0:T(1,128)S(1)} %bitcast.11), custom_call_target="tpu_custom_call" | custom-call | tf_op jit(solution)/shard_map/reduce/pallas_call | solution.py:288
  69.2 0.0 copy-done.1
  69.2 65.0 %chol.1 = (f32[2,128,2,128]{3,2,1,0:T(2,128)}, f32[16,128]{1,0:T(8,128)}) custom-call(s32[16,35]{1,0:T(8,128)S(1)} %copy-done.1, f32[9216,256]{1,0:T(8,128)S(1)} %reduce.1.mat_ref), custom_call_target="tpu_custom_call" | custom-call | tf_op jit(solution)/shard_map/chol/pallas_call | solution.py:575
Async XLA Ops:
  0.6 68.6 %copy-start.1 = (s32[16,35]{1,0:T(8,128)S(1)}, s32[16,35]{1,0:T(8,128)}, u32[]{:S(2)}) copy-start(s32[16,35]{1,0:T(8,128)} %constant.2.clone.plan_ref) | copy-start | bytes 6724
  2.1 0.7 copy-start
  2.8 0.7 copy-start.2

commit v6 on v5

--- a/solution.py
+++ b/solution.py
@@ -17,9 +17,9 @@
 MESH = pl.DeviceIdType.MESH
 ROUNDS = 3
 SKEW = 1
-RED_MB = 34
+RED_MB = 35
 CHOL_MB = 44
-STAGES = 10
+STAGES = 9
 STREAMS = 3 * ROUNDS
 DIAG = [(j, j) for j in range(NS)]
 SIDE = [(i, j) for j in range(NS) for i in range(j + 1, NS)]
@@ -27,7 +27,7 @@
 ROWS = len(TILES) * SB
 HALF = ROWS // 2
 PART = HALF // STREAMS
-UNITS_OF = (PART // 4, PART // 16, PART // 64)
+UNITS_OF = (PART // 4, PART // 16)
 ORDERS = ("xyz", "yzx", "zxy")
 
 
@@ -56,7 +56,7 @@
     return (lax.rem(y, 2) * 4 + x, z * 2 + core, y // 2)
 
 
-def reduce_kernel(scale, blk_ref, coef_ref, res_ref, pay, design, flipped, outbox, inbox, work, near, far, swap_sem, rs_sem, ag_sem, end_sem):
+def reduce_kernel(scale, blk_ref, coef_ref, res_ref, pay, design, flipped, outbox, inbox, work, near, far, ring, swap_sem, rs_sem, ag_sem, end_sem):
     gx, gy, gz = lax.axis_index("gx"), lax.axis_index("gy"), lax.axis_index("gz")
     at = {"x": lax.rem(gx, 4), "y": gz * 2 + gx // 4, "z": gy // 2}
     core = lax.rem(gy, 2)
@@ -182,26 +182,33 @@
             for copy in self.wait:
                 copy.wait_recv()
             self.base = self.pieces[p](0)
-            goal = (pay, mine + self.base) if p == 2 else None
             srcs = tuple(far.at[self.s, k] for k in range(len(self.wait)))
-            add(work, self.base, srcs, sum(UNITS_OF[:p]), UNITS_OF[p], goal)
-
-        def exchange(self, p):
-            self.finish(p - 1)
-            s, unit, piece, axis = self.s, UNITS_OF[p], self.enter(p), self.order[p]
-            off = sum(UNITS_OF[:p])
+            add(work, self.base, srcs, sum(UNITS_OF[:p]), UNITS_OF[p])
+
+        def exchange(self):
+            self.finish(0)
+            s, unit, piece, axis = self.s, UNITS_OF[1], self.enter(1), self.order[1]
+            off = UNITS_OF[0]
             self.wait = tuple(
-                remote(work.at[ds(piece(i), unit)], far.at[s, i - 1, ds(off, unit)], rs_sem.at[s, p, i - 1], device(axis, i))
+                remote(work.at[ds(piece(i), unit)], far.at[s, i - 1, ds(off, unit)], rs_sem.at[s, 1, i - 1], device(axis, i))
                 for i in (1, 2, 3)
             )
 
+        def share(self):
+            self.finish(1)
+            s, unit, axis = self.s, UNITS_OF[1], self.order[2]
+            own = work.at[ds(self.base, unit)]
+            ring[s, at[axis]] = own[...]
+            self.wait = tuple(
+                remote(own, ring.at[s, at[axis]], rs_sem.at[s, 2, i - 1], device(axis, i)) for i in (1, 2, 3)
+            )
+
         def spread(self, p):
             s, unit, axis, piece = self.s, UNITS_OF[p], self.order[p], self.pieces[p]
-            if p == 2:
-                self.finish(2)
-            else:
-                for copy in self.wait:
-                    copy.wait_recv()
+            for copy in self.wait:
+                copy.wait_recv()
+            if p == 1:
+                pay[ds(mine + self.base, unit), :] = ((ring[s, 0] + ring[s, 1]) + ring[s, 2]) + ring[s, 3]
             own = pay.at[ds(mine + piece(0), unit)]
             shifts = (1, 2, 3) if p else (1, 3)
             self.wait = tuple(remote(own, own, ag_sem.at[s, p, i - 1], device(axis, i)) for i in shifts)
@@ -238,13 +245,15 @@
                 self.opposite()
             elif stage == 1:
                 self.sides()
-            elif stage < 4:
-                self.exchange(stage - 1)
-            elif stage < 7:
-                self.spread(6 - stage)
+            elif stage == 2:
+                self.exchange()
+            elif stage == 3:
+                self.share()
+            elif stage < 6:
+                self.spread(5 - stage)
+            elif stage == 6:
+                self.relay()
             elif stage == 7:
-                self.relay()
-            elif stage == 8:
                 self.tail()
             else:
                 self.end()
@@ -298,6 +307,7 @@
             pltpu.VMEM((HALF, SB), F32),
             pltpu.VMEM((STREAMS, UNITS_OF[0], SB), F32),
             pltpu.VMEM((STREAMS, 3, units, SB), F32),
+            pltpu.VMEM((STREAMS, 4, UNITS_OF[1], SB), F32),
             pltpu.SemaphoreType.DMA((STREAMS, 2)),
             pltpu.SemaphoreType.DMA((STREAMS, 3, 4, 2)),
             pltpu.SemaphoreType.DMA((STREAMS, 3, 4, 2)),
@@ -310,14 +320,14 @@
     )(blocks.T, coefficients.reshape(obs, -1), residuals.reshape(1, obs))
 
 
-SPLITS = (6, 12, 16)
+SPLITS = (5, 10, 16)
 DUMMY = G + EXTRA
 TALL = DUMMY + SB + EXTRA
 SEGMENTS = ((0, 8, 7, 7), (8, 14, 3, 6), (14, 16, 1, 0))
 UNITS = 7
 SOLVES = 2
 LAG = 2
-FIRST_UNIT = 6
+UNIT_AT = (9, 9, 9, 10, 10, 10, 11)
 SIDES = NS - 1
 
 
@@ -499,14 +509,15 @@
             for t in range(sides):
                 if t // SOLVES + LAG == g:
                     update_side(t)
-            if FIRST_UNIT <= g < FIRST_UNIT + count:
-                tile_update(g - FIRST_UNIT)
+            for t in range(count):
+                if UNIT_AT[t] == g:
+                    tile_update(t)
 
         block = a_ref[pl.ds(at, BS), cols]
         w = eliminate([block[8 * i : 8 * i + 8] for i in range(BS // 8)], fill)
         w = jnp.concatenate(w, axis=0)
         inv = jnp.where(lane2 <= sub2, w, 0.0)
-        inv_ref[pl.ds(at, BS), :] = inv
+        inv_ref[pl.ds(at, BS), :] = w
         ih, il = split(inv)
         winv_ref[...] = stacked(ih, il)
 
@@ -531,7 +542,6 @@
         def _():
             put(ext, cols, solved([ext], cols))
 
-        a_ref[pl.ds(at, BS), cols] = jnp.where(lane2 == sub2, 1.0 / w, jnp.where(lane2 > sub2, w, 0.0)).T
         return carry
 
     for first, last, sides, count in SEGMENTS:
@@ -544,7 +554,7 @@
         k = n - 1 - s
         at = aligned(k * BS, BS)
         cols = pl.ds(at, BS)
-        z = jnp.sum(column(y_ref[0:1, cols]) * inv_ref[pl.ds(at, BS), :], axis=0, keepdims=True)
+        z = jnp.sum(column(y_ref[0:1, cols]) * jnp.where(lane2 <= sub2, inv_ref[pl.ds(at, BS), :], 0.0), axis=0, keepdims=True)
         sol_ref[pl.ds(k, 1), :] = z
         zc = column(z)
 
@@ -568,7 +578,12 @@
             rows = pl.ds(aligned(rb * BS, BS), BS)
             cols = pl.ds(aligned(cb * BS, BS), BS)
             off = hi_ref[rows, cols].astype(F32) + lo_ref[rows, cols].astype(F32)
-            out_ref[r, :, c, :] = jnp.where(rb > cb, off, jnp.where(rb == cb, a_ref[rows, cols], 0.0))
+            out_ref[r, :, c, :] = jnp.where(rb > cb, off, 0.0)
+
+        @pl.when(p == q)
+        def _(r=r):
+            w = inv_ref[pl.ds(aligned((r * 8 + p) * BS, BS), BS), :]
+            out_ref[r, :, r, :] = jnp.where(lane2 == sub2, 1.0 / w, jnp.where(lane2 > sub2, w, 0.0)).T
 
 
 def cholesky_call(payload):

time: 134 us -> 129 us (0.963)
  Pallas kernels: 131 us -> 125 us
    pallas_call x1, Pallas kernels: 65 us -> 60.6 us  [cholesky_call(): pl.pallas_call(chol_kernel, out_shape=(jax.ShapeDtypeStruct((2, BS, 2, BS...]
where the time goes in v6:
time: 129 us
  Pallas kernels  125 us (97%)
  local copies, waits for them, and re-layouts  2.82 us (2%)
    pallas_call x1, Pallas kernels, reduce_call(): pl.pallas_call(functools.partial(reduce_kernel, scale), out_shape=jax.Sha...  64.8 us
    pallas_call x1, Pallas kernels, cholesky_call(): pl.pallas_call(chol_kernel, out_shape=(jax.ShapeDtypeStruct((2, BS, 2, BS...  60.6 us
    unnamed x7, local copies, waits for them, and re-layouts  2.82 us

profile of v6, /device:TPU:1, one launch (start us, length us, event | category | flops | bytes accessed | tf_op | source)
XLA Modules:
  0.0 128.9 jit_solution(4102062559926112156)
XLA Ops:
  0.6 0.0 copy-start.1
  0.6 1.4 %copy.9 = bf16[128,8,4,128]{3,1,2,0:T(8,128)(2,1)S(1)} copy(bf16[128,8,4,128]{3,2,1,0:T(4,128)(2,1)} %bitcast.12) | data formatting | bytes 2097152
  2.1 0.0 copy-start
  2.1 0.7 copy-done
  2.8 0.0 copy-start.2
  2.8 0.7 copy-done.2
  3.5 64.8 %reduce.1.mat_ref = f32[9216,256]{1,0:T(8,128)S(1)} custom-call(s32[4,1024]{1,0:T(4,128)S(1)} %bitcast.10, bf16[1024,512]{1,0:T(8,128)(2,1)S(1)} %bitcast.9, f32[1,1024]{1,0:T(1,128)S(1)} %bitcast.11), custom_call_target="tpu_custom_call" | custom-call | tf_op jit(solution)/shard_map/reduce/pallas_call | solution.py:297
  68.3 0.0 copy-done.1
  68.3 60.6 %chol.1 = (f32[2,128,2,128]{3,2,1,0:T(2,128)}, f32[16,128]{1,0:T(8,128)}) custom-call(s32[16,35]{1,0:T(8,128)S(1)} %copy-done.1, f32[9216,256]{1,0:T(8,128)S(1)} %reduce.1.mat_ref), custom_call_target="tpu_custom_call" | custom-call | tf_op jit(solution)/shard_map/chol/pallas_call | solution.py:590
Async XLA Ops:
  0.6 67.7 %copy-start.1 = (s32[16,35]{1,0:T(8,128)S(1)}, s32[16,35]{1,0:T(8,128)}, u32[]{:S(2)}) copy-start(s32[16,35]{1,0:T(8,128)} %constant.2.clone.plan_ref) | copy-start | bytes 6724
  2.1 0.7 copy-start
  2.8 0.7 copy-start.2

commit v7 on v6

--- a/solution.py
+++ b/solution.py
@@ -323,7 +323,7 @@
 SPLITS = (5, 10, 16)
 DUMMY = G + EXTRA
 TALL = DUMMY + SB + EXTRA
-SEGMENTS = ((0, 8, 7, 7), (8, 14, 3, 6), (14, 16, 1, 0))
+SEGMENTS = ((0, 2, 7, 0), (2, 8, 6, 7), (8, 14, 3, 6), (14, 16, 1, 0))
 UNITS = 7
 SOLVES = 2
 LAG = 2

time: 129 us -> 128 us (level)
  no operation moved by 1% of the time
where the time goes in v7:
time: 128 us
  Pallas kernels  125 us (98%)
  local copies, waits for them, and re-layouts  2.82 us (2%)
    pallas_call x1, Pallas kernels, reduce_call(): pl.pallas_call(functools.partial(reduce_kernel, scale), out_shape=jax.Sha...  64.8 us
    pallas_call x1, Pallas kernels, cholesky_call(): pl.pallas_call(chol_kernel, out_shape=(jax.ShapeDtypeStruct((2, BS, 2, BS...  59.8 us
    unnamed x7, local copies, waits for them, and re-layouts  2.82 us

profile of v7, /device:TPU:1, one launch (start us, length us, event | category | flops | bytes accessed | tf_op | source)
XLA Modules:
  0.0 128.1 jit_solution(16610852216855075546)
XLA Ops:
  0.6 0.0 copy-start.1
  0.6 1.4 %copy.9 = bf16[128,8,4,128]{3,1,2,0:T(8,128)(2,1)S(1)} copy(bf16[128,8,4,128]{3,2,1,0:T(4,128)(2,1)} %bitcast.12) | data formatting | bytes 2097152
  2.1 0.0 copy-start
  2.1 0.7 copy-done
  2.8 0.0 copy-start.2
  2.8 0.7 copy-done.2
  3.5 64.8 %reduce.1.mat_ref = f32[9216,256]{1,0:T(8,128)S(1)} custom-call(s32[4,1024]{1,0:T(4,128)S(1)} %bitcast.10, bf16[1024,512]{1,0:T(8,128)(2,1)S(1)} %bitcast.9, f32[1,1024]{1,0:T(1,128)S(1)} %bitcast.11), custom_call_target="tpu_custom_call" | custom-call | tf_op jit(solution)/shard_map/reduce/pallas_call | solution.py:297
  68.3 0.0 copy-done.1
  68.3 59.8 %chol.1 = (f32[2,128,2,128]{3,2,1,0:T(2,128)}, f32[16,128]{1,0:T(8,128)}) custom-call(s32[16,35]{1,0:T(8,128)S(1)} %copy-done.1, f32[9216,256]{1,0:T(8,128)S(1)} %reduce.1.mat_ref), custom_call_target="tpu_custom_call" | custom-call | tf_op jit(solution)/shard_map/chol/pallas_call | solution.py:590
Async XLA Ops:
  0.6 67.7 %copy-start.1 = (s32[16,35]{1,0:T(8,128)S(1)}, s32[16,35]{1,0:T(8,128)}, u32[]{:S(2)}) copy-start(s32[16,35]{1,0:T(8,128)} %constant.2.clone.plan_ref) | copy-start | bytes 6724
  2.1 0.7 copy-start
  2.8 0.7 copy-start.2
